TPU v7x, 32 devices: a whole 2x2x4 slice. The times are simulated.
32 devices in a mesh: dp: 2 (over x), tp: 4 (over z), pp: 4 (over y, core).
Axes of the slice: x: 2, y: 2, z: 4, core: 2. Of those that a mesh axis runs over, the one named last changes fastest.
Arguments:
- x_in: bfloat16 [8, 2, 512, 768], P('dp'), parts along dimension 0
- seq_len: int32 [8, 2], P('dp'), parts along dimension 0
- dy_out: bfloat16 [8, 2, 512, 768], P('dp'), parts along dimension 0
- ln1_gain: float32 [4, 768], P('pp')
- ln1_bias: float32 [4, 768], P('pp')
- w_qkv: bfloat16 [4, 3, 768, 12, 64], P('pp', None, None, 'tp')
- b_qkv: float32 [4, 3, 12, 64], P('pp', None, 'tp')
- w_attn: bfloat16 [4, 12, 64, 768], P('pp', 'tp')
- b_attn: float32 [4, 768], P('pp')
- ln2_gain: float32 [4, 768], P('pp')
- ln2_bias: float32 [4, 768], P('pp')
- w_up: bfloat16 [4, 768, 3072], P('pp', None, 'tp')
- b_up: float32 [4, 3072], P('pp', 'tp')
- w_down: bfloat16 [4, 3072, 768], P('pp', 'tp')
- b_down: float32 [4, 768], P('pp')
Outputs:
- output 1: bfloat16 [4, 8, 2, 512, 768], P('pp', 'dp'), parts along dimension 1
- output 2: bfloat16 [4, 8, 2, 512, 768], P('pp', 'dp'), parts along dimension 1
- output 3: float32 [8, 768], P(('dp', 'pp')), parts along dimension 0
- output 4: float32 [8, 768], P(('dp', 'pp')), parts along dimension 0
- output 5: float32 [8, 3, 768, 12, 64], P(('dp', 'pp'), None, None, 'tp'), parts along dimension 0
- output 6: float32 [8, 3, 12, 64], P(('dp', 'pp'), None, 'tp'), parts along dimension 0
- output 7: float32 [8, 12, 64, 768], P(('dp', 'pp'), 'tp'), parts along dimension 0
- output 8: float32 [8, 768], P(('dp', 'pp')), parts along dimension 0
- output 9: float32 [8, 768], P(('dp', 'pp')), parts along dimension 0
- output 10: float32 [8, 768], P(('dp', 'pp')), parts along dimension 0
- output 11: float32 [8, 768, 3072], P(('dp', 'pp'), None, 'tp'), parts along dimension 0
- output 12: float32 [8, 3072], P(('dp', 'pp'), 'tp'), parts along dimension 0
- output 13: float32 [8, 3072, 768], P(('dp', 'pp'), 'tp'), parts along dimension 0
- output 14: float32 [8, 768], P(('dp', 'pp')), parts along dimension 0
There are 2 independent parts. A program takes and returns all parts, laid end to end along the dimension named above; an argument that names none is the same for every part.
All inputs are finite; a program needn't handle non-finite values.
Results may differ from a plain program's by a relative error of at most 0.02.
Values are sent between devices in bfloat16 or wider.
A program may use at most 1 GiB of HBM per device.

v0:
```python
import jax
import jax.numpy as jnp
import functools
from jax import lax
from jax.sharding import PartitionSpec as P

LN_EPS = 1e-5
MASK_VALUE = -1e9


def layer_norm(h_f32, ln_gain, ln_bias):
    row_mean = jnp.mean(h_f32, axis=-1, keepdims=True)
    centred = h_f32 - row_mean
    row_var = jnp.mean(centred * centred, axis=-1, keepdims=True)
    return centred * lax.rsqrt(row_var + LN_EPS) * ln_gain + ln_bias


def attention_core(normed, w_qkv, b_qkv, key_ok):
    qkv_bf = (jnp.einsum('bsd,tdhk->tbshk', normed, w_qkv, preferred_element_type=jnp.float32) + b_qkv[:, None, None]).astype(jnp.bfloat16)
    inv_sqrt = qkv_bf.shape[-1] ** -0.5
    scores = jnp.einsum('bqhk,bshk->bhqs', qkv_bf[0], qkv_bf[1], preferred_element_type=jnp.float32) * inv_sqrt
    scores = jnp.where(key_ok[:, None, None, :], scores, MASK_VALUE)
    prob_f32 = jax.nn.softmax(scores, axis=-1)
    prob_bf = prob_f32.astype(jnp.bfloat16)
    context = jnp.einsum('bhqs,bshk->bqhk', prob_bf, qkv_bf[2], preferred_element_type=jnp.float32).astype(jnp.bfloat16)
    return qkv_bf, prob_f32, prob_bf, context


def layer_forward(h_in, params, key_ok):
    (ln1_gain, ln1_bias, w_qkv, b_qkv, w_attn, b_attn, ln2_gain, ln2_bias, w_up, b_up, w_down, b_down) = params
    x_f32 = h_in.astype(jnp.float32)
    normed = layer_norm(x_f32, ln1_gain, ln1_bias).astype(jnp.bfloat16)
    context = attention_core(normed, w_qkv, b_qkv, key_ok)[3]
    attn_sum = lax.psum(jnp.einsum('cril,ile->cre', context, w_attn, preferred_element_type=jnp.float32).astype(jnp.bfloat16), 'tp')
    mid_act = (x_f32 + attn_sum.astype(jnp.float32) + b_attn).astype(jnp.bfloat16)
    normed2 = layer_norm(mid_act.astype(jnp.float32), ln2_gain, ln2_bias).astype(jnp.bfloat16)
    hidden = jax.nn.gelu(jnp.einsum('bsd,df->bsf', normed2, w_up, preferred_element_type=jnp.float32) + b_up, approximate=False).astype(jnp.bfloat16)
    down_sum = lax.psum(jnp.einsum('bsf,fd->bsd', hidden, w_down, preferred_element_type=jnp.float32).astype(jnp.bfloat16), 'tp')
    out_act = (mid_act.astype(jnp.float32) + down_sum.astype(jnp.float32) + b_down).astype(jnp.bfloat16)
    return mid_act, out_act


def layer_backward(h_in, mid_act, g_out, params, key_ok):
    (ln1_gain, ln1_bias, w_qkv, b_qkv, w_attn, b_attn, ln2_gain, ln2_bias, w_up, b_up, w_down, b_down) = params
    normed_f32, ln1_back = jax.vjp(layer_norm, h_in.astype(jnp.float32), ln1_gain, ln1_bias)
    normed = normed_f32.astype(jnp.bfloat16)
    qkv_bf, prob_f32, prob_bf, context = attention_core(normed, w_qkv, b_qkv, key_ok)
    normed2_f32, ln2_back = jax.vjp(layer_norm, mid_act.astype(jnp.float32), ln2_gain, ln2_bias)
    normed2 = normed2_f32.astype(jnp.bfloat16)
    up_f32 = jnp.einsum('bsd,df->bsf', normed2, w_up, preferred_element_type=jnp.float32) + b_up
    hidden_f32, gelu_back = jax.vjp(functools.partial(jax.nn.gelu, approximate=False), up_f32)
    hidden = hidden_f32.astype(jnp.bfloat16)

    grad_w_down = jnp.einsum('bsf,bsd->fd', hidden, g_out, preferred_element_type=jnp.float32)
    grad_b_down = jnp.sum(g_out, axis=(0, 1), dtype=jnp.float32)
    d_hidden = jnp.einsum('bsd,fd->bsf', g_out, w_down, preferred_element_type=jnp.float32).astype(jnp.bfloat16)
    d_up = gelu_back(d_hidden.astype(jnp.float32))[0]
    d_up_bf = d_up.astype(jnp.bfloat16)
    grad_w_up = jnp.einsum('bsd,bsf->df', normed2, d_up_bf, preferred_element_type=jnp.float32)
    grad_b_up = jnp.sum(d_up, axis=(0, 1))
    d_normed2 = lax.psum(jnp.einsum('bsf,df->bsd', d_up_bf, w_up, preferred_element_type=jnp.float32).astype(jnp.bfloat16), 'tp')
    d_mid_ln, grad_ln2_gain, grad_ln2_bias = ln2_back(d_normed2.astype(jnp.float32))
    d_mid = (g_out.astype(jnp.float32) + d_mid_ln).astype(jnp.bfloat16)

    grad_w_attn = jnp.einsum('cril,cre->ile', context, d_mid, preferred_element_type=jnp.float32)
    grad_b_attn = jnp.sum(d_mid, axis=(0, 1), dtype=jnp.float32)
    d_context = jnp.einsum('cre,ile->cril', d_mid, w_attn, preferred_element_type=jnp.float32).astype(jnp.bfloat16)
    d_probs = jnp.einsum('bqhk,bshk->bhqs', d_context, qkv_bf[2], preferred_element_type=jnp.float32)
    d_values = jnp.einsum('bhqs,bqhk->bshk', prob_bf, d_context, preferred_element_type=jnp.float32)
    inv_sqrt = qkv_bf.shape[-1] ** -0.5
    d_scores = (prob_f32 * (d_probs - jnp.sum(d_probs * prob_f32, axis=-1, keepdims=True)) * inv_sqrt).astype(jnp.bfloat16)
    d_query = jnp.einsum('bhqs,bshk->bqhk', d_scores, qkv_bf[1], preferred_element_type=jnp.float32)
    d_keys = jnp.einsum('bhqs,bqhk->bshk', d_scores, qkv_bf[0], preferred_element_type=jnp.float32)
    d_qkv = jnp.stack([d_query.astype(jnp.bfloat16), d_keys.astype(jnp.bfloat16), d_values.astype(jnp.bfloat16)])
    grad_w_qkv = jnp.einsum('bsd,tbshk->tdhk', normed, d_qkv, preferred_element_type=jnp.float32)
    grad_b_qkv = jnp.sum(d_qkv, axis=(1, 2), dtype=jnp.float32)
    d_normed = lax.psum(jnp.einsum('tbshk,tdhk->bsd', d_qkv, w_qkv, preferred_element_type=jnp.float32).astype(jnp.bfloat16), 'tp')
    d_x_ln, grad_ln1_gain, grad_ln1_bias = ln1_back(d_normed.astype(jnp.float32))
    d_x = (d_mid.astype(jnp.float32) + d_x_ln).astype(jnp.bfloat16)
    return d_x, (grad_ln1_gain, grad_ln1_bias, grad_w_qkv, grad_b_qkv, grad_w_attn, grad_b_attn, grad_ln2_gain, grad_ln2_bias, grad_w_up, grad_b_up, grad_w_down, grad_b_down)


def store_slot(buffer, new_val, slot_idx, is_valid):
    old_val = lax.dynamic_index_in_dim(buffer, slot_idx, 0, keepdims=False)
    return lax.dynamic_update_index_in_dim(buffer, jnp.where(is_valid, new_val, old_val), slot_idx, 0)


def solution(mesh):
    n_stages = mesh.shape['pp']
    fwd_pairs = [(src, src + 1) for src in range(n_stages - 1)]
    bwd_pairs = [(src + 1, src) for src in range(n_stages - 1)]
    act_spec = P('dp', None, None, None)
    param_specs = (P('pp', None), P('pp', None), P('pp', None, None, 'tp', None), P('pp', None, 'tp', None), P('pp', 'tp', None, None), P('pp', None), P('pp', None), P('pp', None), P('pp', None, 'tp'), P('pp', 'tp'), P('pp', 'tp', None), P('pp', None))
    group_axes = ('dp', 'pp')
    grad_specs = (P(group_axes, None), P(group_axes, None), P(group_axes, None, None, 'tp', None), P(group_axes, None, 'tp', None), P(group_axes, 'tp', None, None), P(group_axes, None), P(group_axes, None), P(group_axes, None), P(group_axes, None, 'tp'), P(group_axes, 'tp'), P(group_axes, 'tp', None), P(group_axes, None))
    stage_spec = P('pp', 'dp', None, None, None)

    def stage_body(x_in, seq_len, dy_out, *weights):
        params = tuple(weight[0] for weight in weights)
        stage_id = lax.axis_index('pp')
        n_micro = x_in.shape[0]
        key_ok = jnp.arange(x_in.shape[2])[None, None, :] < seq_len[:, :, None]
        n_steps = n_micro + n_stages - 1
        zero_act = jnp.zeros(x_in.shape[1:], x_in.dtype)
        act_buf = jnp.zeros_like(x_in)

        def fwd_step(state, step_idx):
            recv_act, in_buf, mid_buf, out_buf = state
            micro_idx = step_idx - stage_id
            is_valid = (micro_idx >= 0) & (micro_idx < n_micro)
            slot_idx = jnp.clip(micro_idx, 0, n_micro - 1)
            first_in = lax.dynamic_index_in_dim(x_in, jnp.minimum(step_idx, n_micro - 1), 0, keepdims=False)
            h_in = jnp.where(stage_id == 0, first_in, recv_act)
            ok_micro = lax.dynamic_index_in_dim(key_ok, slot_idx, 0, keepdims=False)
            mid_act, out_act = layer_forward(h_in, params, ok_micro)
            in_buf = store_slot(in_buf, h_in, slot_idx, is_valid)
            mid_buf = store_slot(mid_buf, mid_act, slot_idx, is_valid)
            out_buf = store_slot(out_buf, out_act, slot_idx, is_valid)
            recv_act = lax.ppermute(out_act, 'pp', fwd_pairs)
            return (recv_act, in_buf, mid_buf, out_buf), None

        fwd_state, _ = lax.scan(fwd_step, (zero_act, act_buf, act_buf, act_buf), jnp.arange(n_steps))
        in_buf, mid_buf, out_buf = fwd_state[1], fwd_state[2], fwd_state[3]
        zero_grads = tuple(jnp.zeros(param.shape, jnp.float32) for param in params)

        def bwd_step(state, step_idx):
            recv_grad, dx_buf, grad_sum = state
            micro_idx = step_idx - (n_stages - 1 - stage_id)
            is_valid = (micro_idx >= 0) & (micro_idx < n_micro)
            slot_idx = jnp.clip(micro_idx, 0, n_micro - 1)
            top_grad = lax.dynamic_index_in_dim(dy_out, jnp.minimum(step_idx, n_micro - 1), 0, keepdims=False)
            top_grad = jnp.where(step_idx < n_micro, top_grad, jnp.zeros_like(top_grad))
            g_out = jnp.where(stage_id == n_stages - 1, top_grad, recv_grad)
            h_in = lax.dynamic_index_in_dim(in_buf, slot_idx, 0, keepdims=False)
            mid_act = lax.dynamic_index_in_dim(mid_buf, slot_idx, 0, keepdims=False)
            ok_micro = lax.dynamic_index_in_dim(key_ok, slot_idx, 0, keepdims=False)
            dx_act, grad_step = layer_backward(h_in, mid_act, g_out, params, ok_micro)
            grad_sum = tuple(acc + new_grad for acc, new_grad in zip(grad_sum, grad_step))
            dx_buf = store_slot(dx_buf, dx_act, slot_idx, is_valid)
            recv_grad = lax.ppermute(dx_act, 'pp', bwd_pairs)
            return (recv_grad, dx_buf, grad_sum), None

        bwd_state, _ = lax.scan(bwd_step, (zero_act, act_buf, zero_grads), jnp.arange(n_steps))
        dx_buf, grad_sum = bwd_state[1], bwd_state[2]
        return (out_buf[None], dx_buf[None]) + tuple(grad[None] for grad in grad_sum)

    return jax.shard_map(stage_body, mesh=mesh, in_specs=(act_spec, P('dp', None), act_spec) + param_specs, out_specs=(stage_spec, stage_spec) + grad_specs, check_vma=False)
```

profile of v0, /device:TPU:1, one launch (start us, length us, event | category | flops | bytes accessed | tf_op | source)
XLA Modules:
  0.0 3216.1 jit_solution(5573492764422642994)
XLA Ops:
  23.0 1436.3 %while.56 = (s32[]{:T(128)}, bf16[2,512,768]{2,1,0:T(8,128)(2,1)}, bf16[4,2,512,768]{3,2,1,0:T(8,128)(2,1)}, bf16[4,2,512,768]{3,2,1,0:T(8,128)(2,1)}, bf16[4,2,...) while((s32[]{:T(128)}, bf16[2,512,768]{2,1,0:T(8,128)(2,1)}, ...), condition=%wide.region_9.10_spmd, body=%wide.region_0.9_spmd.sunk | while | flops 4136438272 | bytes 107132248 | solution.py:122
  49.8 65.9 %all-reduce.5.cloned.1.call-done = bf16[2,512,768]{2,1,0:T(8,128)(2,1)} async-done(((bf16[2,512,768]{2,1,0:T(8,128)(2,1)}), bf16[2,512,768]{2,1,0:T(8,128)(2,1)}) %all-reduce.5.cloned.1.call-update) | async-done | bytes 1572880 | tf_op jit(solution)/shard_map/while/body/eval_jaxpr/psum | solution.py:34
  136.7 66.9 %all-reduce.7.cloned.1.call-done = bf16[2,512,768]{2,1,0:T(8,128)(2,1)} async-done(((bf16[2,512,768]{2,1,0:T(8,128)(2,1)}), bf16[2,512,768]{2,1,0:T(8,128)(2,1)}) %all-reduce.7.cloned.1.call-update) | async-done | bytes 1572880 | tf_op jit(solution)/shard_map/while/body/eval_jaxpr/psum | solution.py:38
  256.6 64.2 %all-reduce.5.cloned.1.call-done = bf16[2,512,768]{2,1,0:T(8,128)(2,1)} async-done(((bf16[2,512,768]{2,1,0:T(8,128)(2,1)}), bf16[2,512,768]{2,1,0:T(8,128)(2,1)}) %all-reduce.5.cloned.1.call-update) | async-done | bytes 1572880 | tf_op jit(solution)/shard_map/while/body/eval_jaxpr/psum | solution.py:34
  341.7 66.9 %all-reduce.7.cloned.1.call-done = bf16[2,512,768]{2,1,0:T(8,128)(2,1)} async-done(((bf16[2,512,768]{2,1,0:T(8,128)(2,1)}), bf16[2,512,768]{2,1,0:T(8,128)(2,1)}) %all-reduce.7.cloned.1.call-update) | async-done | bytes 1572880 | tf_op jit(solution)/shard_map/while/body/eval_jaxpr/psum | solution.py:38
  461.5 64.2 %all-reduce.5.cloned.1.call-done = bf16[2,512,768]{2,1,0:T(8,128)(2,1)} async-done(((bf16[2,512,768]{2,1,0:T(8,128)(2,1)}), bf16[2,512,768]{2,1,0:T(8,128)(2,1)}) %all-reduce.5.cloned.1.call-update) | async-done | bytes 1572880 | tf_op jit(solution)/shard_map/while/body/eval_jaxpr/psum | solution.py:34
  546.7 66.9 %all-reduce.7.cloned.1.call-done = bf16[2,512,768]{2,1,0:T(8,128)(2,1)} async-done(((bf16[2,512,768]{2,1,0:T(8,128)(2,1)}), bf16[2,512,768]{2,1,0:T(8,128)(2,1)}) %all-reduce.7.cloned.1.call-update) | async-done | bytes 1572880 | tf_op jit(solution)/shard_map/while/body/eval_jaxpr/psum | solution.py:38
  666.5 64.1 %all-reduce.5.cloned.1.call-done = bf16[2,512,768]{2,1,0:T(8,128)(2,1)} async-done(((bf16[2,512,768]{2,1,0:T(8,128)(2,1)}), bf16[2,512,768]{2,1,0:T(8,128)(2,1)}) %all-reduce.5.cloned.1.call-update) | async-done | bytes 1572880 | tf_op jit(solution)/shard_map/while/body/eval_jaxpr/psum | solution.py:34
  751.6 66.9 %all-reduce.7.cloned.1.call-done = bf16[2,512,768]{2,1,0:T(8,128)(2,1)} async-done(((bf16[2,512,768]{2,1,0:T(8,128)(2,1)}), bf16[2,512,768]{2,1,0:T(8,128)(2,1)}) %all-reduce.7.cloned.1.call-update) | async-done | bytes 1572880 | tf_op jit(solution)/shard_map/while/body/eval_jaxpr/psum | solution.py:38
  871.3 64.2 %all-reduce.5.cloned.1.call-done = bf16[2,512,768]{2,1,0:T(8,128)(2,1)} async-done(((bf16[2,512,768]{2,1,0:T(8,128)(2,1)}), bf16[2,512,768]{2,1,0:T(8,128)(2,1)}) %all-reduce.5.cloned.1.call-update) | async-done | bytes 1572880 | tf_op jit(solution)/shard_map/while/body/eval_jaxpr/psum | solution.py:34
  956.5 67.0 %all-reduce.7.cloned.1.call-done = bf16[2,512,768]{2,1,0:T(8,128)(2,1)} async-done(((bf16[2,512,768]{2,1,0:T(8,128)(2,1)}), bf16[2,512,768]{2,1,0:T(8,128)(2,1)}) %all-reduce.7.cloned.1.call-update) | async-done | bytes 1572880 | tf_op jit(solution)/shard_map/while/body/eval_jaxpr/psum | solution.py:38
  1076.3 64.1 %all-reduce.5.cloned.1.call-done = bf16[2,512,768]{2,1,0:T(8,128)(2,1)} async-done(((bf16[2,512,768]{2,1,0:T(8,128)(2,1)}), bf16[2,512,768]{2,1,0:T(8,128)(2,1)}) %all-reduce.5.cloned.1.call-update) | async-done | bytes 1572880 | tf_op jit(solution)/shard_map/while/body/eval_jaxpr/psum | solution.py:34
  1161.4 66.9 %all-reduce.7.cloned.1.call-done = bf16[2,512,768]{2,1,0:T(8,128)(2,1)} async-done(((bf16[2,512,768]{2,1,0:T(8,128)(2,1)}), bf16[2,512,768]{2,1,0:T(8,128)(2,1)}) %all-reduce.7.cloned.1.call-update) | async-done | bytes 1572880 | tf_op jit(solution)/shard_map/while/body/eval_jaxpr/psum | solution.py:38
  1281.2 64.1 %all-reduce.5.cloned.1.call-done = bf16[2,512,768]{2,1,0:T(8,128)(2,1)} async-done(((bf16[2,512,768]{2,1,0:T(8,128)(2,1)}), bf16[2,512,768]{2,1,0:T(8,128)(2,1)}) %all-reduce.5.cloned.1.call-update) | async-done | bytes 1572880 | tf_op jit(solution)/shard_map/while/body/eval_jaxpr/psum | solution.py:34
  1366.3 66.9 %all-reduce.7.cloned.1.call-done = bf16[2,512,768]{2,1,0:T(8,128)(2,1)} async-done(((bf16[2,512,768]{2,1,0:T(8,128)(2,1)}), bf16[2,512,768]{2,1,0:T(8,128)(2,1)}) %all-reduce.7.cloned.1.call-update) | async-done | bytes 1572880 | tf_op jit(solution)/shard_map/while/body/eval_jaxpr/psum | solution.py:38
  1463.7 1735.7 %while.57 = (s32[]{:T(128)}, bf16[2,512,768]{2,1,0:T(8,128)(2,1)}, bf16[4,2,512,768]{3,2,1,0:T(8,128)(2,1)}, f32[768]{0:T(1024)}, f32[768]{0:T(1024)}, /*index=5...) while((s32[]{:T(128)}, bf16[2,512,768]{2,1,0:T(8,128)(2,1)}, ...), condition=%wide.region_32.33_spmd.clone, body=%wide.region_10.32_spmd.clone.sunk | while | flops 10778275840 | bytes 338714624 | solution.py:143
  1537.2 47.8 %all-reduce.9.cloned.1.call-done = bf16[2,512,768]{2,1,0:T(8,128)(2,1)} async-done(((bf16[2,512,768]{2,1,0:T(8,128)(2,1)}), bf16[2,512,768]{2,1,0:T(8,128)(2,1)}) %all-reduce.9.cloned.1.call-update) | async-done | bytes 1572880 | tf_op jit(solution)/shard_map/while/body/eval_jaxpr/psum | solution.py:61
  1637.7 60.2 %all-reduce.11.cloned.1.call-done = bf16[2,512,768]{2,1,0:T(8,128)(2,1)} async-done(((bf16[2,512,768]{2,1,0:T(8,128)(2,1)}), bf16[2,512,768]{2,1,0:T(8,128)(2,1)}) %all-reduce.11.cloned.1.call-update) | async-done | bytes 1572880 | tf_op jit(solution)/shard_map/while/body/eval_jaxpr/psum | solution.py:77
  1883.1 59.5 %all-reduce.11.cloned.1.call-done = bf16[2,512,768]{2,1,0:T(8,128)(2,1)} async-done(((bf16[2,512,768]{2,1,0:T(8,128)(2,1)}), bf16[2,512,768]{2,1,0:T(8,128)(2,1)}) %all-reduce.11.cloned.1.call-update) | async-done | bytes 1572880 | tf_op jit(solution)/shard_map/while/body/eval_jaxpr/psum | solution.py:77
  2127.7 59.5 %all-reduce.11.cloned.1.call-done = bf16[2,512,768]{2,1,0:T(8,128)(2,1)} async-done(((bf16[2,512,768]{2,1,0:T(8,128)(2,1)}), bf16[2,512,768]{2,1,0:T(8,128)(2,1)}) %all-reduce.11.cloned.1.call-update) | async-done | bytes 1572880 | tf_op jit(solution)/shard_map/while/body/eval_jaxpr/psum | solution.py:77
  2372.2 59.5 %all-reduce.11.cloned.1.call-done = bf16[2,512,768]{2,1,0:T(8,128)(2,1)} async-done(((bf16[2,512,768]{2,1,0:T(8,128)(2,1)}), bf16[2,512,768]{2,1,0:T(8,128)(2,1)}) %all-reduce.11.cloned.1.call-update) | async-done | bytes 1572880 | tf_op jit(solution)/shard_map/while/body/eval_jaxpr/psum | solution.py:77
  2616.8 59.5 %all-reduce.11.cloned.1.call-done = bf16[2,512,768]{2,1,0:T(8,128)(2,1)} async-done(((bf16[2,512,768]{2,1,0:T(8,128)(2,1)}), bf16[2,512,768]{2,1,0:T(8,128)(2,1)}) %all-reduce.11.cloned.1.call-update) | async-done | bytes 1572880 | tf_op jit(solution)/shard_map/while/body/eval_jaxpr/psum | solution.py:77
  2861.4 59.5 %all-reduce.11.cloned.1.call-done = bf16[2,512,768]{2,1,0:T(8,128)(2,1)} async-done(((bf16[2,512,768]{2,1,0:T(8,128)(2,1)}), bf16[2,512,768]{2,1,0:T(8,128)(2,1)}) %all-reduce.11.cloned.1.call-update) | async-done | bytes 1572880 | tf_op jit(solution)/shard_map/while/body/eval_jaxpr/psum | solution.py:77
  3106.0 59.5 %all-reduce.11.cloned.1.call-done = bf16[2,512,768]{2,1,0:T(8,128)(2,1)} async-done(((bf16[2,512,768]{2,1,0:T(8,128)(2,1)}), bf16[2,512,768]{2,1,0:T(8,128)(2,1)}) %all-reduce.11.cloned.1.call-update) | async-done | bytes 1572880 | tf_op jit(solution)/shard_map/while/body/eval_jaxpr/psum | solution.py:77
  (1313 shorter events, 1767.2 us)
Async XLA Ops:
  23.0 92.8 %all-reduce.5.cloned.1.call-start = ((), (), s32[]{:S(2)}) async-start(), calls=%async_computation | async-start | bytes 3145728 | tf_op jit(solution)/shard_map/while/body/eval_jaxpr/psum | solution.py:34
  45.0 158.6 %all-reduce.7.cloned.1.call-start = ((), (), s32[]{:S(2)}) async-start(), calls=%async_computation.1 | async-start | bytes 3145728 | tf_op jit(solution)/shard_map/while/body/eval_jaxpr/psum | solution.py:38
  229.8 91.0 %all-reduce.5.cloned.1.call-start = ((), (), s32[]{:S(2)}) async-start(), calls=%async_computation | async-start | bytes 3145728 | tf_op jit(solution)/shard_map/while/body/eval_jaxpr/psum | solution.py:34
  251.8 156.9 %all-reduce.7.cloned.1.call-start = ((), (), s32[]{:S(2)}) async-start(), calls=%async_computation.1 | async-start | bytes 3145728 | tf_op jit(solution)/shard_map/while/body/eval_jaxpr/psum | solution.py:38
  434.7 91.0 %all-reduce.5.cloned.1.call-start = ((), (), s32[]{:S(2)}) async-start(), calls=%async_computation | async-start | bytes 3145728 | tf_op jit(solution)/shard_map/while/body/eval_jaxpr/psum | solution.py:34
  456.6 157.0 %all-reduce.7.cloned.1.call-start = ((), (), s32[]{:S(2)}) async-start(), calls=%async_computation.1 | async-start | bytes 3145728 | tf_op jit(solution)/shard_map/while/body/eval_jaxpr/psum | solution.py:38
  661.6 156.8 %all-reduce.7.cloned.1.call-start = ((), (), s32[]{:S(2)}) async-start(), calls=%async_computation.1 | async-start | bytes 3145728 | tf_op jit(solution)/shard_map/while/body/eval_jaxpr/psum | solution.py:38
  866.5 156.9 %all-reduce.7.cloned.1.call-start = ((), (), s32[]{:S(2)}) async-start(), calls=%async_computation.1 | async-start | bytes 3145728 | tf_op jit(solution)/shard_map/while/body/eval_jaxpr/psum | solution.py:38
  1071.5 156.8 %all-reduce.7.cloned.1.call-start = ((), (), s32[]{:S(2)}) async-start(), calls=%async_computation.1 | async-start | bytes 3145728 | tf_op jit(solution)/shard_map/while/body/eval_jaxpr/psum | solution.py:38
  1276.4 156.8 %all-reduce.7.cloned.1.call-start = ((), (), s32[]{:S(2)}) async-start(), calls=%async_computation.1 | async-start | bytes 3145728 | tf_op jit(solution)/shard_map/while/body/eval_jaxpr/psum | solution.py:38
  1485.2 99.8 %all-reduce.9.cloned.1.call-start = ((), (), s32[]{:S(2)}) async-start(), calls=%async_computation.2 | async-start | bytes 3145728 | tf_op jit(solution)/shard_map/while/body/eval_jaxpr/psum | solution.py:61
  1516.0 182.0 %all-reduce.11.cloned.1.call-start = ((), (), s32[]{:S(2)}) async-start(), calls=%async_computation.3 | async-start | bytes 3145728 | tf_op jit(solution)/shard_map/while/body/eval_jaxpr/psum | solution.py:77
  1731.9 97.6 %all-reduce.9.cloned.1.call-start = ((), (), s32[]{:S(2)}) async-start(), calls=%async_computation.2 | async-start | bytes 3145728 | tf_op jit(solution)/shard_map/while/body/eval_jaxpr/psum | solution.py:61
  1762.8 179.8 %all-reduce.11.cloned.1.call-start = ((), (), s32[]{:S(2)}) async-start(), calls=%async_computation.3 | async-start | bytes 3145728 | tf_op jit(solution)/shard_map/while/body/eval_jaxpr/psum | solution.py:77
  1976.5 97.6 %all-reduce.9.cloned.1.call-start = ((), (), s32[]{:S(2)}) async-start(), calls=%async_computation.2 | async-start | bytes 3145728 | tf_op jit(solution)/shard_map/while/body/eval_jaxpr/psum | solution.py:61
  2007.4 179.8 %all-reduce.11.cloned.1.call-start = ((), (), s32[]{:S(2)}) async-start(), calls=%async_computation.3 | async-start | bytes 3145728 | tf_op jit(solution)/shard_map/while/body/eval_jaxpr/psum | solution.py:77
  2221.1 97.6 %all-reduce.9.cloned.1.call-start = ((), (), s32[]{:S(2)}) async-start(), calls=%async_computation.2 | async-start | bytes 3145728 | tf_op jit(solution)/shard_map/while/body/eval_jaxpr/psum | solution.py:61
  2251.9 179.8 %all-reduce.11.cloned.1.call-start = ((), (), s32[]{:S(2)}) async-start(), calls=%async_computation.3 | async-start | bytes 3145728 | tf_op jit(solution)/shard_map/while/body/eval_jaxpr/psum | solution.py:77
  2465.7 97.6 %all-reduce.9.cloned.1.call-start = ((), (), s32[]{:S(2)}) async-start(), calls=%async_computation.2 | async-start | bytes 3145728 | tf_op jit(solution)/shard_map/while/body/eval_jaxpr/psum | solution.py:61
  2496.5 179.8 %all-reduce.11.cloned.1.call-start = ((), (), s32[]{:S(2)}) async-start(), calls=%async_computation.3 | async-start | bytes 3145728 | tf_op jit(solution)/shard_map/while/body/eval_jaxpr/psum | solution.py:77
  2710.3 97.6 %all-reduce.9.cloned.1.call-start = ((), (), s32[]{:S(2)}) async-start(), calls=%async_computation.2 | async-start | bytes 3145728 | tf_op jit(solution)/shard_map/while/body/eval_jaxpr/psum | solution.py:61
  2741.1 179.8 %all-reduce.11.cloned.1.call-start = ((), (), s32[]{:S(2)}) async-start(), calls=%async_computation.3 | async-start | bytes 3145728 | tf_op jit(solution)/shard_map/while/body/eval_jaxpr/psum | solution.py:77
  2954.9 97.6 %all-reduce.9.cloned.1.call-start = ((), (), s32[]{:S(2)}) async-start(), calls=%async_computation.2 | async-start | bytes 3145728 | tf_op jit(solution)/shard_map/while/body/eval_jaxpr/psum | solution.py:61
  2985.7 179.8 %all-reduce.11.cloned.1.call-start = ((), (), s32[]{:S(2)}) async-start(), calls=%async_computation.3 | async-start | bytes 3145728 | tf_op jit(solution)/shard_map/while/body/eval_jaxpr/psum | solution.py:77
  (330 other events, 4791.5 us)
Sparse Core Ops, SparseCore 0:
  45.1 70.6 all-reduce.4
  135.3 68.2 all-reduce.6
  251.9 68.8 all-reduce.4
  340.3 68.2 all-reduce.6
  456.7 68.9 all-reduce.4
  545.3 68.2 all-reduce.6
  661.8 68.7 all-reduce.4
  750.1 68.2 all-reduce.6
  866.6 68.8 all-reduce.4
  955.0 68.3 all-reduce.6
  1071.6 68.8 all-reduce.4
  1160.0 68.2 all-reduce.6
  1276.5 68.8 all-reduce.4
  1364.9 68.2 all-reduce.6
  1516.1 68.8 all-reduce.8
  1629.7 68.2 all-reduce.10
  1762.9 66.6 all-reduce.8
  1874.2 68.2 all-reduce.10
  2007.5 66.6 all-reduce.8
  2118.8 68.2 all-reduce.10
  2363.4 68.2 all-reduce.10
  2608.0 68.2 all-reduce.10
  2852.6 68.2 all-reduce.10
  3097.2 68.2 all-reduce.10
  (4 shorter events, 266.4 us)
where the time goes:
time: 3230 us; the launch traced here: 3220 us
  waiting for transfers between devices  1850 us (57%)
  matrix products  695 us (22%)
  other arithmetic  432 us (13%)
  local copies, waits for them, and re-layouts  129 us (4%)
  loops' own time  50.2 us (2%)
  starting transfers between devices  47.6 us (1%)
    psum x7, waiting for transfers between devices, layer_forward(): lax.psum(jnp.einsum('bsf,fd->bsd', hidden, w_down, preferred_element_type...  468 us
    psum x7, waiting for transfers between devices, layer_forward(): lax.psum(jnp.einsum('cril,ile->cre', context, w_attn, preferred_element_t...  451 us
    psum x7, waiting for transfers between devices, layer_backward(): lax.psum(jnp.einsum('tbshk,tdhk->bsd', d_qkv, w_qkv, preferred_element_ty...  417 us
    psum x7, waiting for transfers between devices, layer_backward(): lax.psum(jnp.einsum('bsf,df->bsd', d_up_bf, w_up, preferred_element_type=...  317 us
    ppermute x7, waiting for transfers between devices, fwd_step(): recv_act = lax.ppermute(out_act, 'pp', fwd_pairs)  121 us
    dynamic_update_slice x28, other arithmetic, store_slot(): lax.dynamic_update_index_in_dim(buffer, jnp.where(is_valid, new_val, old_...  113 us
    reduce_sum x28, other arithmetic, layer_norm(): return centred * lax.rsqrt(row_var + LN_EPS) * ln_gain + ln_bias  101 us
    dot_general x7, matrix products, layer_forward(): jnp.einsum('bsf,fd->bsd', hidden, w_down, preferred_element_type=jnp.floa...  76.5 us
  transfers between devices with their start and end apart: 42, of which 42 were waited for; matrix products, arithmetic and copies ran while one was open for 10% of the time, Pallas kernels for 0%

commit v1 on v0

v1 whole, which is shorter than its diff:
```python
import functools

import jax
import jax.numpy as jnp
from jax import lax
from jax.experimental import pallas as pl
from jax.experimental.pallas import tpu as pltpu
from jax.sharding import Mesh, PartitionSpec as P

LN_EPS = 1e-5
MASK_VALUE = -1e9
F32 = jnp.float32
BF16 = jnp.bfloat16
NT = (((1,), (1,)), ((), ()))
NN = (((1,), (0,)), ((), ()))
TN = (((0,), (0,)), ((), ()))


def dot(lhs, rhs, dims):
    return lax.dot_general(lhs, rhs, dims, preferred_element_type=F32)


def attn_fwd_kernel(len_ref, q_ref, k_ref, v_ref, ctx_ref):
    rows = q_ref.shape[0]
    key_ok = lax.broadcasted_iota(jnp.int32, (rows, rows), 1) < len_ref[0]
    parts = []
    for half in range(2):
        cols = slice(half * 64, half * 64 + 64)
        scores = dot(q_ref[:, cols], k_ref[:, cols], NT) * 0.125
        scores = jnp.where(key_ok, scores, MASK_VALUE)
        expd = jnp.exp(scores - jnp.max(scores, axis=-1, keepdims=True))
        prob = (expd * (1.0 / jnp.sum(expd, axis=-1, keepdims=True))).astype(BF16)
        parts.append(dot(prob, v_ref[:, cols], NN).astype(BF16))
    ctx_ref[...] = jnp.concatenate(parts, axis=1)


def attn_bwd_kernel(len_ref, q_ref, k_ref, v_ref, dctx_ref, dqkv_ref):
    rows = q_ref.shape[0]
    width = dqkv_ref.shape[1] // 3
    key_ok = lax.broadcasted_iota(jnp.int32, (rows, rows), 0) < len_ref[0]
    pieces = ([], [], [])
    for half in range(2):
        cols = slice(half * 64, half * 64 + 64)
        q, k, v, dctx = q_ref[:, cols], k_ref[:, cols], v_ref[:, cols], dctx_ref[:, cols]
        scores = dot(k, q, NT) * 0.125
        scores = jnp.where(key_ok, scores, MASK_VALUE)
        expd = jnp.exp(scores - jnp.max(scores, axis=0, keepdims=True))
        prob = expd * (1.0 / jnp.sum(expd, axis=0, keepdims=True))
        d_prob = dot(v, dctx, NT)
        delta = jnp.sum(d_prob * prob, axis=0, keepdims=True)
        d_scores = (prob * (d_prob - delta) * 0.125).astype(BF16)
        pieces[0].append(dot(d_scores, k, TN).astype(BF16))
        pieces[1].append(dot(d_scores, q, NN).astype(BF16))
        pieces[2].append(dot(prob.astype(BF16), dctx, NN).astype(BF16))
    pair = pl.program_id(0)
    for part in range(3):
        start = pl.multiple_of(part * width + pair * 128, 128)
        dqkv_ref[:, pl.ds(start, 128)] = jnp.concatenate(pieces[part], axis=1)


def col_spec(rows, offset):
    return pl.BlockSpec((rows, 128), lambda i: (0, offset + i))


SMEM_SPEC = pl.BlockSpec(memory_space=pltpu.SMEM)


def attn_fwd(qkv, length):
    rows, width = qkv.shape[0], qkv.shape[1] // 3
    pairs = width // 128
    return pl.pallas_call(
        attn_fwd_kernel,
        grid=(pairs,),
        out_shape=jax.ShapeDtypeStruct((rows, width), BF16),
        in_specs=[SMEM_SPEC] + [col_spec(rows, part * pairs) for part in range(3)],
        out_specs=col_spec(rows, 0),
        cost_estimate=pl.CostEstimate(flops=8 * pairs * rows * rows * 64 * 4, bytes_accessed=8 * rows * width, transcendentals=2 * pairs * rows * rows),
        name='attn_fwd',
    )(length, qkv, qkv, qkv)


def attn_bwd(qkv, dctx, length):
    rows, width = qkv.shape[0], qkv.shape[1] // 3
    pairs = width // 128
    return pl.pallas_call(
        attn_bwd_kernel,
        grid=(pairs,),
        out_shape=jax.ShapeDtypeStruct((rows, 3 * width), BF16),
        in_specs=[SMEM_SPEC] + [col_spec(rows, part * pairs) for part in range(3)] + [col_spec(rows, 0)],
        out_specs=pl.BlockSpec((rows, 3 * width), lambda i: (0, 0)),
        cost_estimate=pl.CostEstimate(flops=20 * pairs * rows * rows * 64 * 4, bytes_accessed=14 * rows * width, transcendentals=2 * pairs * rows * rows),
        name='attn_bwd',
    )(length, qkv, qkv, qkv, dctx)


def normalise(v_bf):
    v = v_bf.astype(F32)
    centred = v - jnp.mean(v, axis=-1, keepdims=True)
    rstd = lax.rsqrt(jnp.mean(centred * centred, axis=-1, keepdims=True) + LN_EPS)
    return centred * rstd, rstd


def layer_norm(v_bf, gain, bias):
    return (normalise(v_bf)[0] * gain + bias).astype(BF16)


def norm_back(v_bf, gain, d_out_bf, residual_bf):
    xhat, rstd = normalise(v_bf)
    d_out = d_out_bf.astype(F32)
    d_hat = d_out * gain
    d_in = rstd * (d_hat - jnp.mean(d_hat, axis=-1, keepdims=True) - xhat * jnp.mean(d_hat * xhat, axis=-1, keepdims=True))
    d_v = (residual_bf.astype(F32) + d_in).astype(BF16)
    return d_v, jnp.sum(d_out * xhat, axis=0), jnp.sum(d_out, axis=0)


def gelu(value):
    return jax.nn.gelu(value, approximate=False)


def gelu_back(up, d_hidden_bf):
    return jax.vjp(gelu, up)[1](d_hidden_bf.astype(F32))[0]


def layer_forward(h_in, params, length):
    w_att, w_up, w_down, vec, b_qkv, b_up = params
    n_qkv = b_qkv.shape[0]
    normed = layer_norm(h_in, vec[0], vec[1])
    qkv = (dot(normed, w_att[:n_qkv], NT) + b_qkv).astype(BF16)
    context = attn_fwd(qkv, length)
    mid = (h_in.astype(F32) + dot(context, w_att[n_qkv:], NN) + vec[2]).astype(BF16)
    normed2 = layer_norm(mid, vec[3], vec[4])
    up = dot(normed2, w_up, NT) + b_up
    hidden = gelu(up).astype(BF16)
    out = (mid.astype(F32) + dot(hidden, w_down, NN) + vec[5]).astype(BF16)
    return out, (h_in, normed, qkv, context, mid, up)


def layer_backward(g_out, saved, params, length):
    w_att, w_up, w_down, vec, b_qkv, b_up = params
    n_qkv = b_qkv.shape[0]
    h_in, normed, qkv, context, mid, up = saved
    d_hidden = dot(g_out, w_down, NT).astype(BF16)
    d_up = gelu_back(up, d_hidden).astype(BF16)
    d_normed2 = dot(d_up, w_up, NN).astype(BF16)
    d_mid, d_gain2, d_bias2 = norm_back(mid, vec[3], d_normed2, g_out)
    d_context = dot(d_mid, w_att[n_qkv:], NT).astype(BF16)
    d_qkv = attn_bwd(qkv, d_context, length)
    d_normed = dot(d_qkv, w_att[:n_qkv], NN).astype(BF16)
    d_x, d_gain1, d_bias1 = norm_back(h_in, vec[0], d_normed, d_mid)
    d_b_attn = jnp.sum(d_mid, axis=0, dtype=F32)
    d_b_qkv = jnp.sum(d_qkv, axis=0, dtype=F32).reshape(3, -1)
    small = jnp.concatenate([jnp.stack([d_gain1, d_bias1, d_b_attn, d_gain2, d_bias2]), d_b_qkv])
    return d_x, (d_qkv, d_mid, context, normed, small)


def solution(mesh):
    n_dp, n_tp, n_pp = mesh.shape['dp'], mesh.shape['tp'], mesh.shape['pp']
    split = Mesh(mesh.devices.reshape(n_dp, n_tp, n_pp // 2, 2), ('dp', 'tp', 'py', 'core'))
    pp = ('py', 'core')
    act_spec = P('dp', None, None, None)
    param_specs = (P(pp, None), P(pp, None), P(pp, None, None, 'tp', None), P(pp, None, 'tp', None), P(pp, 'tp', None, None), P(pp, None), P(pp, None), P(pp, None), P(pp, None, 'tp'), P(pp, 'tp'), P(pp, 'tp', None), P(pp, None))
    gp = ('dp', 'py', 'core')
    grad_specs = (P(gp, None), P(gp, None), P(gp, None, None, 'tp', None), P(gp, None, 'tp', None), P(gp, 'tp', None, None), P(gp, None), P(gp, None), P(gp, None), P(gp, None, 'tp'), P(gp, 'tp'), P(gp, 'tp', None), P(gp, None))
    stage_spec = P(pp, 'dp', None, None, None)
    swap = [(0, 1), (1, 0)]

    def body(x_in, seq_len, dy_out, *weights):
        (ln1_gain, ln1_bias, w_qkv, b_qkv, w_attn, b_attn, ln2_gain, ln2_bias, w_up, b_up, w_down, b_down) = tuple(weight[0] for weight in weights)
        dp_id, tp_id, py_id, core_id = (lax.axis_index(name) for name in ('dp', 'tp', 'py', 'core'))
        n_micro, _, rows, width = x_in.shape
        n_local = w_attn.shape[0] * w_attn.shape[1]
        first_core, first_pair = core_id == 0, py_id == 0

        def gather_weight(shard):
            half = shard.shape[0] // n_dp
            piece = lax.dynamic_slice_in_dim(shard, dp_id * half, half, 0)
            return lax.all_gather(piece, ('tp', 'dp'), axis=0, tiled=True)

        att_shard = jnp.concatenate([w_qkv.reshape(3, width, n_local).transpose(0, 2, 1).reshape(3 * n_local, width), w_attn.reshape(n_local, width)])
        att_full = gather_weight(att_shard).reshape(n_tp, 4, n_local, width).transpose(1, 0, 2, 3).reshape(4 * n_tp * n_local, width)
        up_full = gather_weight(w_up.T)
        down_full = gather_weight(w_down)
        both = [lax.all_gather(full, 'core', axis=0) for full in (att_full, up_full, down_full)]

        b_qkv_flat = b_qkv.reshape(3 * n_local)
        packed = jnp.concatenate([jnp.stack([ln1_gain, ln1_bias, b_attn, ln2_gain, ln2_bias, b_down]), jnp.pad(b_qkv_flat, (0, width - 3 * n_local))[None], b_up.reshape(-1, width)])
        packed = lax.all_gather(packed, ('core', 'tp'), axis=0).reshape(2, n_tp, -1, width)

        def layer_params(layer):
            b_qkv_full = packed[layer, :, 6, :3 * n_local].reshape(n_tp, 3, n_local).transpose(1, 0, 2).reshape(-1)
            b_up_full = packed[layer, :, 7:].reshape(-1)
            return tuple(arr[layer] for arr in both) + (packed[layer, 0, :6], b_qkv_full, b_up_full)

        params = (layer_params(0), layer_params(1))

        def my_sequence(array):
            return lax.dynamic_slice(array, (tp_id, core_id, 0, 0), (1, 1, rows, width)).reshape(rows, width)

        length = lax.dynamic_slice(seq_len, (tp_id, core_id), (1, 1)).reshape(1)

        def forward(h):
            mid, saved0 = layer_forward(h, params[0], length)
            out, saved1 = layer_forward(mid, params[1], length)
            return (mid, out), (saved0, saved1)

        def backward(g, saved):
            dx1, keep1 = layer_backward(g, saved[1], params[1], length)
            dx0, keep0 = layer_backward(dx1, saved[0], params[0], length)
            return (dx0, dx1), (keep0, keep1)

        outs_a, saved_a = forward(my_sequence(x_in))
        outs_b, saved_b = forward(lax.ppermute(outs_a[1], 'py', [(0, 1)]))

        def own_stage(phase0, phase1):
            by_layer = [jnp.where(first_pair, phase0[layer], phase1[layer]) for layer in range(2)]
            keep = jnp.where(first_core, by_layer[0], by_layer[1])
            other = lax.ppermute(jnp.where(first_core, by_layer[1], by_layer[0]), 'core', swap)
            return jnp.stack([jnp.where(first_core, keep, other), jnp.where(first_core, other, keep)])

        def gather_tokens(phase0, phase1):
            return lax.all_gather(own_stage(phase0, phase1), 'tp', axis=0)

        stage_out = gather_tokens(outs_a, outs_b)
        mid_all = gather_tokens([saved[4] for saved in saved_a], [saved[4] for saved in saved_b])

        dxs_b, keeps_b = backward(my_sequence(dy_out), saved_b)
        dxs_a, keeps_a = backward(lax.ppermute(dxs_b[0], 'py', [(1, 0)]), saved_a)

        stage_dx = gather_tokens(dxs_a, dxs_b)
        next_dx = lax.ppermute(stage_dx, pp, [(s + 1, s) for s in range(n_pp - 1)])
        is_last = (~first_pair) & (~first_core)
        g_all = jnp.where(is_last, dy_out, next_dx).reshape(-1, width)

        d_qkv, d_mid, context, normed, small = (own_stage([keep[i] for keep in keeps_a], [keep[i] for keep in keeps_b]) for i in range(5))
        tokens = 2 * rows
        gw_qkv = dot(d_qkv.reshape(tokens, -1), normed.reshape(tokens, -1), TN)
        gw_attn = dot(context.reshape(tokens, -1), d_mid.reshape(tokens, -1), TN)
        small = small[0] + small[1]
        gw_att = jnp.concatenate([gw_qkv, gw_attn]).reshape(4, n_tp, n_local, width).transpose(1, 0, 2, 3).reshape(n_tp, 4 * n_local, width)
        gb_qkv = small[5:].reshape(3, n_tp, n_local).transpose(1, 0, 2).reshape(n_tp, 1, 3 * n_local)
        gb_qkv = jnp.pad(gb_qkv, ((0, 0), (0, 2), (0, width - 3 * n_local)))
        payload = jnp.concatenate([gw_att, jnp.broadcast_to(small[None, :5], (n_tp, 5, width)), gb_qkv], axis=1)
        reduced = lax.psum_scatter(payload, 'tp', scatter_dimension=0, tiled=False)
        g_qkv = reduced[:3 * n_local].reshape(3, n_local, width).transpose(0, 2, 1).reshape(w_qkv.shape)
        g_attn = reduced[3 * n_local:4 * n_local].reshape(w_attn.shape)
        g_vec = reduced[4 * n_local:]

        mid_flat = mid_all.reshape(-1, width)
        normed2 = layer_norm(mid_flat, ln2_gain, ln2_bias)
        up = dot(normed2, w_up, NN) + b_up
        hidden = gelu(up).astype(BF16)
        d_hidden = dot(g_all, w_down, NT).astype(BF16)
        d_up = gelu_back(up, d_hidden)
        g_w_up = dot(normed2, d_up.astype(BF16), TN)
        g_w_down = dot(hidden, g_all, TN)
        g_b_up = jnp.sum(d_up, axis=0)
        g_b_down = jnp.sum(g_all, axis=0, dtype=F32)

        grads = (g_vec[0], g_vec[1], g_qkv, g_vec[5, :3 * n_local].reshape(b_qkv.shape), g_attn, g_vec[2], g_vec[3], g_vec[4], g_w_up, g_b_up, g_w_down, g_b_down)
        return (stage_out[None], stage_dx[None]) + tuple(grad[None] for grad in grads)

    return jax.shard_map(body, mesh=split, in_specs=(act_spec, P('dp', None), act_spec) + param_specs, out_specs=(stage_spec, stage_spec) + grad_specs, check_vma=False)
```

time: 3230 us -> 1140 us (0.35)
  waiting for transfers between devices: 1850 us -> 458 us
  matrix products: 695 us -> 321 us
  other arithmetic: 432 us -> 97.1 us
  Pallas kernels: 0 us -> 129 us
  local copies, waits for them, and re-layouts: 129 us -> 69.9 us
  loops' own time: 50.2 us -> 0 us
  starting transfers between devices: 47.6 us -> 11.7 us
    psum x28 -> x0, waiting for transfers between devices: 1650 us -> none  [the longest x7 468 us: layer_forward(): lax.psum(jnp.einsum('bsf,fd->bsd', hidden, w_down, preferred_element_type...]
    all_gather x0 -> x9, waiting for transfers between devices: none -> 358 us  [the longest x3 235 us: gather_weight(): return lax.all_gather(piece, ('tp', 'dp'), axis=0, tiled=True)]
    dot_general x126 -> x38, matrix products: 636 us -> 321 us  [dot(): return lax.dot_general(lhs, rhs, dims, preferred_element_type=F32)]
    reduce_sum x98 -> x21, other arithmetic: 200 us -> 35.6 us  [the longest x9 8.67 us: normalise(): jnp.mean(centred * centred, axis=-1, keepdims=True) + LN_EPS]
    ppermute x14 -> x11, waiting for transfers between devices: 193 us -> 59.4 us  [the longest x1 29 us: body(): next_dx = lax.ppermute(stage_dx, pp, [(s + 1, s) for s in range(n_pp - 1)])]
    pallas_call x0 -> x8, Pallas kernels: none -> 129 us  [the longest x4 76.5 us: attn_bwd(): pl.pallas_call(attn_bwd_kernel, grid=(pairs,), out_shape=jax.ShapeDtypeSt...]
    dynamic_update_slice x28 -> x0, other arithmetic: 113 us -> none  [store_slot(): lax.dynamic_update_index_in_dim(buffer, jnp.where(is_valid, new_val, old_...]
    dynamic_slice x42 -> x3, local copies, waits for them, and re-layouts: 68.1 us -> 3.46 us  [the longest x2 2.81 us: gather_weight(): piece = lax.dynamic_slice_in_dim(shard, dp_id * half, half, 0)]
  transfers between devices with their start and end apart: 42 -> 21, of which waited for: 42 -> 12; matrix products, arithmetic and copies ran while one was open for 10% -> 30% of each run, Pallas kernels for 0% -> 6%
where the time goes in v1:
time: 1140 us; the launch traced here: 1130 us
  waiting for transfers between devices  458 us (40%)
  matrix products  321 us (28%)
  Pallas kernels  129 us (11%)
  other arithmetic  97.1 us (9%)
  local copies, waits for them, and re-layouts  69.9 us (6%)
  blocking collectives  25.1 us (2%)
  between operations  16.6 us (1%)
  starting transfers between devices  11.7 us (1%)
    dot_general x38, matrix products, dot(): return lax.dot_general(lhs, rhs, dims, preferred_element_type=F32)  321 us
    all_gather x3, waiting for transfers between devices, gather_weight(): return lax.all_gather(piece, ('tp', 'dp'), axis=0, tiled=True)  235 us
    all_gather x3, waiting for transfers between devices, gather_tokens(): return lax.all_gather(own_stage(phase0, phase1), 'tp', axis=0)  120 us
    pallas_call x4, Pallas kernels, attn_bwd(): pl.pallas_call(attn_bwd_kernel, grid=(pairs,), out_shape=jax.ShapeDtypeSt...  76.5 us
    pallas_call x4, Pallas kernels, attn_fwd(): pl.pallas_call(attn_fwd_kernel, grid=(pairs,), out_shape=jax.ShapeDtypeSt...  52.9 us
    reduce_scatter x1, waiting for transfers between devices, body(): reduced = lax.psum_scatter(payload, 'tp', scatter_dimension=0, tiled=False)  40.3 us
    ppermute x1, waiting for transfers between devices, body(): next_dx = lax.ppermute(stage_dx, pp, [(s + 1, s) for s in range(n_pp - 1)])  29 us
    all_gather x1, blocking collectives, body(): lax.all_gather(packed, ('core', 'tp'), axis=0).reshape(2, n_tp, -1, width)  25.1 us
  transfers between devices with their start and end apart: 21, of which 12 were waited for; matrix products, arithmetic and copies ran while one was open for 30% of the time, Pallas kernels for 6%

profile of v1, /device:TPU:1, one launch (start us, length us, event | category | flops | bytes accessed | tf_op | source)
XLA Modules:
  0.0 1129.1 jit_solution(8501189016539786636)
XLA Ops:
  12.6 78.0 %all-gather.17.cloned.1.call-done = bf16[3072,768]{1,0:T(8,128)(2,1)} async-done(((bf16[384,768]{1,0:T(8,128)(2,1)}), bf16[3072,768]{1,0:T(8,128)(2,1)}) %all-gather.17.cloned.1.call-update) | async-done | bytes 4718608 | tf_op jit(solution)/shard_map/all_gather | solution.py:177
  95.7 76.8 %all-gather.21.cloned.1.call-done = bf16[3072,768]{0,1:T(8,128)(2,1)} async-done(((bf16[384,768]{0,1:T(8,128)(2,1)}), bf16[3072,768]{0,1:T(8,128)(2,1)}) %all-gather.21.cloned.1.call-update) | async-done | bytes 4718608 | tf_op jit(solution)/shard_map/all_gather | solution.py:177
  172.5 79.9 %all-gather.25.cloned.1.call-done = bf16[1,3072,768]{2,1,0:T(8,128)(2,1)} async-done(((bf16[1,384,768]{2,1,0:T(8,128)(2,1)}), bf16[1,3072,768]{2,1,0:T(8,128)(2,1)}) %all-gather.25.cloned.1.call-update) | async-done | bytes 4718608 | tf_op jit(solution)/shard_map/all_gather | solution.py:177
  252.7 25.1 %all-gather = f32[64,768]{1,0:T(8,128)S(1)} all-gather(f32[8,768]{1,0:T(8,128)S(1)} %concatenate.24), channel_id=2, replica_groups=mesh['dp'=2,'tp'=4,'py'=2,'core'=2] {'core','tp'}, dimensions={0}, use_global_device_ids=true | all-gather | bytes 221184 | tf_op jit(solution)/shard_map/all_gather | solution.py:187
  287.9 13.3 %attn_fwd.4 = bf16[512,768]{1,0:T(8,128)(2,1)} custom-call(s32[1]{0:T(128)} %bitcast.1.len_ref, bf16[512,2304]{1,0:T(8,128)(2,1)} %fusion.76.q_ref.k_ref.v_ref, bf16[512,2304]{1,0:T(8,128)(2,1)} %fusion.76.q_ref.k_ref.v_ref, bf16[512,2304]{1,0:T(8,128)(2,1)} %fusion.76.q_ref.k_ref.v_ref), custom_call_target="tpu_custom_call" | custom-call | flops 3221225472 | bytes 3145728 | tf_op jit(solution)/shard_map/attn_fwd/pallas_call | solution.py:71
  304.2 19.9 %fusion.44 = (f32[512,3072]{1,0:T(8,128)}, f32[512,3072]{1,0:T(8,128)}) fusion(f32[3072]{0:T(1024)S(1)} %bitcast.300, bf16[6144,768]{0,1:T(8,128)(2,1)} %all-gather.23.cloned.1.call-done, bf16[512,768]{1,0:T(8,128)(2,1)S(1)} %get-tuple-element.161, f32[768]{0:T(1024)S(1)} %get-tuple-element.95, f32[768]{0:T(1024)S(1)} %get-tuple-element.96, ...), kind=kOutput, calls=%fused_computation.76 | convolution fusion | flops 2517368832 | bytes 18110464 | tf_op jit(solution)/shard_map/dot_general | solution.py:20
  342.3 13.1 %attn_fwd.5 = bf16[512,768]{1,0:T(8,128)(2,1)} custom-call(s32[1]{0:T(128)} %bitcast.1.len_ref, bf16[512,2304]{1,0:T(8,128)(2,1)} %fusion.77.q_ref.k_ref.v_ref, bf16[512,2304]{1,0:T(8,128)(2,1)} %fusion.77.q_ref.k_ref.v_ref, bf16[512,2304]{1,0:T(8,128)(2,1)} %fusion.77.q_ref.k_ref.v_ref), custom_call_target="tpu_custom_call" | custom-call | flops 3221225472 | bytes 3145728 | tf_op jit(solution)/shard_map/attn_fwd/pallas_call | solution.py:71
  358.4 17.9 %fusion.45 = (f32[512,3072]{1,0:T(8,128)S(1)}, f32[512,3072]{1,0:T(8,128)S(1)}) fusion(f32[3072]{0:T(1024)S(1)} %bitcast.306, bf16[6144,768]{0,1:T(8,128)(2,1)} %all-gather.23.cloned.1.call-done, bf16[512,768]{1,0:T(8,128)(2,1)S(1)} %get-tuple-element.167, f32[768]{0:T(1024)S(1)} %get-tuple-element.89, f32[768]{0:T(1024)S(1)} %get-tuple-element.90, ...), kind=kOutput, calls=%fused_computation.77 | convolution fusion | flops 2517368832 | bytes 18110464 | tf_op jit(solution)/shard_map/dot_general | solution.py:20
  407.2 13.3 %attn_fwd.6 = bf16[512,768]{1,0:T(8,128)(2,1)} custom-call(s32[1]{0:T(128)} %bitcast.1.len_ref, bf16[512,2304]{1,0:T(8,128)(2,1)} %fusion.78.q_ref.k_ref.v_ref, bf16[512,2304]{1,0:T(8,128)(2,1)} %fusion.78.q_ref.k_ref.v_ref, bf16[512,2304]{1,0:T(8,128)(2,1)} %fusion.78.q_ref.k_ref.v_ref), custom_call_target="tpu_custom_call" | custom-call | flops 3221225472 | bytes 3145728 | tf_op jit(solution)/shard_map/attn_fwd/pallas_call | solution.py:71
  423.5 18.1 %fusion.46 = (f32[512,3072]{1,0:T(8,128)S(1)}, f32[512,3072]{1,0:T(8,128)S(1)}) fusion(f32[3072]{0:T(1024)S(1)} %bitcast.302, bf16[6144,768]{0,1:T(8,128)(2,1)} %all-gather.23.cloned.1.call-done, bf16[512,768]{1,0:T(8,128)(2,1)S(1)} %get-tuple-element.171, f32[512]{0:T(512)S(1)} %add_rsqrt_fusion.3, f32[512]{0:T(512)S(1)} %broadcast_multiply_fusion.19, ...), kind=kOutput, calls=%fused_computation.78 | convolution fusion | flops 2517368832 | bytes 18110464 | tf_op jit(solution)/shard_map/dot_general | solution.py:20
  452.7 13.1 %attn_fwd.7 = bf16[512,768]{1,0:T(8,128)(2,1)} custom-call(s32[1]{0:T(128)} %bitcast.1.len_ref, bf16[512,2304]{1,0:T(8,128)(2,1)} %fusion.79.q_ref.k_ref.v_ref, bf16[512,2304]{1,0:T(8,128)(2,1)} %fusion.79.q_ref.k_ref.v_ref, bf16[512,2304]{1,0:T(8,128)(2,1)} %fusion.79.q_ref.k_ref.v_ref), custom_call_target="tpu_custom_call" | custom-call | flops 3221225472 | bytes 3145728 | tf_op jit(solution)/shard_map/attn_fwd/pallas_call | solution.py:71
  468.8 20.0 %fusion.47 = (f32[512,3072]{1,0:T(8,128)}, f32[512,3072]{1,0:T(8,128)}) fusion(f32[3072]{0:T(1024)S(1)} %bitcast.309, bf16[6144,768]{0,1:T(8,128)(2,1)} %all-gather.23.cloned.1.call-done, bf16[512,768]{1,0:T(8,128)(2,1)S(1)} %get-tuple-element.177, f32[512]{0:T(512)S(1)} %add_rsqrt_fusion.1, f32[512]{0:T(512)S(1)} %broadcast_multiply_fusion.17, ...), kind=kOutput, calls=%fused_computation.79 | convolution fusion | flops 2517368832 | bytes 18110464 | tf_op jit(solution)/shard_map/dot_general | solution.py:20
  505.6 19.3 %attn_bwd.4 = bf16[512,2304]{1,0:T(8,128)(2,1)} custom-call(s32[1]{0:T(128)} %bitcast.1.len_ref, bf16[512,2304]{1,0:T(8,128)(2,1)} %fusion.79.q_ref.k_ref.v_ref, bf16[512,2304]{1,0:T(8,128)(2,1)} %fusion.79.q_ref.k_ref.v_ref, bf16[512,2304]{1,0:T(8,128)(2,1)} %fusion.79.q_ref.k_ref.v_ref, bf16[512,768]{1,0:T(8,128)(2,1)} %convolution_convert_fusion.8.dctx_ref), custom_call_target="tpu_custom_call" | custom-call | flops 8053063680 | bytes 5505024 | tf_op jit(solution)/shard_map/attn_bwd/pallas_call | solution.py:85
  564.4 19.0 %attn_bwd.5 = bf16[512,2304]{1,0:T(8,128)(2,1)} custom-call(s32[1]{0:T(128)} %bitcast.1.len_ref, bf16[512,2304]{1,0:T(8,128)(2,1)} %fusion.78.q_ref.k_ref.v_ref, bf16[512,2304]{1,0:T(8,128)(2,1)} %fusion.78.q_ref.k_ref.v_ref, bf16[512,2304]{1,0:T(8,128)(2,1)} %fusion.78.q_ref.k_ref.v_ref, bf16[512,768]{1,0:T(8,128)(2,1)} %convolution_convert_fusion.7.dctx_ref), custom_call_target="tpu_custom_call" | custom-call | flops 8053063680 | bytes 5505024 | tf_op jit(solution)/shard_map/attn_bwd/pallas_call | solution.py:85
  595.1 16.9 %collective-permute-done.2 = bf16[512,768]{1,0:T(8,128)(2,1)} collective-permute-done((bf16[512,768]{1,0:T(8,128)(2,1)}, bf16[512,768]{1,0:T(8,128)(2,1)}, u32[]{:S(2)}, u32[]{:S(2)}) %collective-permute-start.2) | collective-permute-done | bytes 786464 | tf_op jit(solution)/shard_map/ppermute | solution.py:227
  635.7 19.2 %attn_bwd.6 = bf16[512,2304]{1,0:T(8,128)(2,1)} custom-call(s32[1]{0:T(128)} %bitcast.1.len_ref, bf16[512,2304]{1,0:T(8,128)(2,1)} %fusion.77.q_ref.k_ref.v_ref, bf16[512,2304]{1,0:T(8,128)(2,1)} %fusion.77.q_ref.k_ref.v_ref, bf16[512,2304]{1,0:T(8,128)(2,1)} %fusion.77.q_ref.k_ref.v_ref, bf16[512,768]{1,0:T(8,128)(2,1)} %convolution_convert_fusion.6.dctx_ref), custom_call_target="tpu_custom_call" | custom-call | flops 8053063680 | bytes 5505024 | tf_op jit(solution)/shard_map/attn_bwd/pallas_call | solution.py:85
  690.0 19.0 %attn_bwd.7 = bf16[512,2304]{1,0:T(8,128)(2,1)} custom-call(s32[1]{0:T(128)} %bitcast.1.len_ref, bf16[512,2304]{1,0:T(8,128)(2,1)} %fusion.76.q_ref.k_ref.v_ref, bf16[512,2304]{1,0:T(8,128)(2,1)} %fusion.76.q_ref.k_ref.v_ref, bf16[512,2304]{1,0:T(8,128)(2,1)} %fusion.76.q_ref.k_ref.v_ref, bf16[512,768]{1,0:T(8,128)(2,1)} %convolution_convert_fusion.5.dctx_ref), custom_call_target="tpu_custom_call" | custom-call | flops 8053063680 | bytes 5505024 | tf_op jit(solution)/shard_map/attn_bwd/pallas_call | solution.py:85
  813.7 13.5 %all-gather.33.cloned.1.call-done = bf16[8,512,768]{2,1,0:T(8,128)(2,1)} async-done(((bf16[2,512,768]{2,1,0:T(8,128)(2,1)}), bf16[8,512,768]{2,1,0:T(8,128)(2,1)}) %all-gather.33.cloned.1.call-update) | async-done | bytes 6291472 | tf_op jit(solution)/shard_map/all_gather | solution.py:221
  835.6 106.6 %all-gather.31.cloned.1.call-done = bf16[8,512,768]{2,1,0:T(8,128)(2,1)} async-done(((bf16[2,512,768]{2,1,0:T(8,128)(2,1)}), bf16[8,512,768]{2,1,0:T(8,128)(2,1)}) %all-gather.31.cloned.1.call-update) | async-done | bytes 6291472 | tf_op jit(solution)/shard_map/all_gather | solution.py:221
  950.1 31.6 %fusion.6 = (f32[4096,768]{1,0:T(8,128)}, f32[4096,768]{1,0:T(8,128)}) fusion(f32[768]{0:T(1024)S(1)} %copy-done.107, bf16[4096,768]{1,0:T(8,128)(2,1)S(1)} %bitcast.285, bf16[1,768,768]{2,1,0:T(8,128)(2,1)S(1)} %copy-done), kind=kOutput, calls=%fused_computation.9 | convolution fusion | flops 5030019072 | bytes 32640000 | tf_op jit(solution)/shard_map/dot_general | solution.py:20
  985.9 29.0 %collective-permute-done.10 = bf16[4,2,512,768]{3,2,1,0:T(8,128)(2,1)} collective-permute-done((bf16[4,2,512,768]{3,2,1,0:T(8,128)(2,1)}, bf16[4,2,512,768]{3,2,1,0:T(8,128)(2,1)}, u32[]{:S(2)}, u32[]{:S(2)}) %collective-permute-start.10) | collective-permute-done | bytes 6291488 | tf_op jit(solution)/shard_map/ppermute | solution.py:230
  1023.4 18.8 %fusion.371 = (f32[768]{0:T(1024)S(1)}, bf16[4096,768]{1,0:T(8,128)(2,1)}) fusion(f32[4096,768]{1,0:T(8,128)} %get-tuple-element.189, bf16[4096,768]{1,0:T(8,128)(2,1)} %bitcast.283, bf16[1,768,768]{2,1,0:T(8,128)(2,1)} %param.28, f32[4096,768]{1,0:T(8,128)} %get-tuple-element.190, f32[768]{0:T(1024)S(1)} %copy-done.107), kind=kOutput, calls=%fused_computation.586 | convolution fusion | flops 4888460288 | bytes 38934528 | tf_op jit(solution)/shard_map/dot_general | solution.py:20
  1052.5 12.4 %fusion.177 = f32[1,768,768]{2,1,0:T(8,128)} fusion(bf16[4096,768]{1,0:T(8,128)(2,1)S(1)} %bitcast.284, f32[4096,768]{1,0:T(8,128)} %get-tuple-element.189, f32[4096,768]{1,0:T(8,128)} %get-tuple-element.190, f32[768]{0:T(1024)S(1)} %copy-done.107), kind=kOutput, calls=%fused_computation.321 | convolution fusion | flops 4844421120 | bytes 33819648 | tf_op jit(solution)/shard_map/dot_general | solution.py:20
  1064.9 40.3 %reduce-scatter.2.cloned.1.call-done = f32[1,776,768]{2,1,0:T(8,128)} async-done(((f32[4,776,768]{2,1,0:T(8,128)}), f32[1,776,768]{2,1,0:T(8,128)}) %reduce-scatter.2.cloned.1.call-update) | async-done | bytes 2383888 | tf_op jit(solution)/shard_map/reduce_scatter | solution.py:243
  (524 shorter events, 378.1 us)
Async XLA Ops:
  7.2 83.4 %all-gather.17.cloned.1.call-start = ((), (), s32[]{:S(2)}) async-start(), calls=%async_computation.1 | async-start | bytes 5308416 | tf_op jit(solution)/shard_map/all_gather | solution.py:177
  9.6 162.9 %all-gather.21.cloned.1.call-start = ((), (), s32[]{:S(2)}) async-start(), calls=%async_computation.3 | async-start | bytes 5308416 | tf_op jit(solution)/shard_map/all_gather | solution.py:177
  10.5 241.9 %all-gather.25.cloned.1.call-start = ((), (), s32[]{:S(2)}) async-start(), calls=%async_computation.6 | async-start | bytes 5308416 | tf_op jit(solution)/shard_map/all_gather | solution.py:177
  12.5 269.5 %all-gather.19.cloned.1.call-start = ((), (), s32[]{:S(2)}) async-start(), calls=%async_computation.2 | async-start | bytes 14155776 | tf_op jit(solution)/shard_map/all_gather | solution.py:183
  95.6 157.1 %copy-start.115 = (f32[1,768]{1,0:T(1,128)S(1)}, f32[1,768]{1,0:T(1,128)}, u32[]{:S(2)}) copy-start(f32[1,768]{1,0:T(1,128)} %param.18) | copy-start | bytes 9220
  95.6 157.1 %copy-start.116 = (f32[1,768]{1,0:T(1,128)S(1)}, f32[1,768]{1,0:T(1,128)}, u32[]{:S(2)}) copy-start(f32[1,768]{1,0:T(1,128)} %param.19) | copy-start | bytes 9220
  95.6 182.6 %copy-start.119 = (s32[4,2]{0,1:T(2,128)S(1)}, s32[4,2]{0,1:T(2,128)}, u32[]{:S(2)}) copy-start(s32[4,2]{0,1:T(2,128)} %param.16) | copy-start | bytes 100
  95.6 208.6 %all-gather.23.cloned.1.call-start = ((), (), s32[]{:S(2)}) async-start(), calls=%async_computation.5 | async-start | bytes 14155776 | tf_op jit(solution)/shard_map/all_gather | solution.py:183
  172.5 155.0 %all-gather.27.cloned.1.call-start = ((), (), s32[]{:S(2)}) async-start(), calls=%async_computation.7 | async-start | bytes 14155776 | tf_op jit(solution)/shard_map/all_gather | solution.py:183
  252.4 561.2 %all-gather.29.cloned.1.call-start = ((), (), s32[]{:S(2)}) async-start(), calls=%async_computation.8 | async-start | bytes 7864320 | tf_op jit(solution)/shard_map/all_gather | solution.py:221
  380.9 20.1 %collective-permute-start = (bf16[512,768]{1,0:T(8,128)(2,1)S(1)}, bf16[512,768]{1,0:T(8,128)(2,1)S(1)}, u32[]{:S(2)}, u32[]{:S(2)}) collective-permute-start(bf16[512,768]{1,0:T(8,128)(2,1)S(1)} %fusion.249), channel_id=1, source_target_pairs={{0,2},{1,3},{4,6},{5,7},{8,10},{9,11},{12,14},{13,15},{16,18},{17,... | collective-permute-start | bytes 2359304 | tf_op jit(solution)/shard_map/ppermute | solution.py:212
  535.5 56.7 %collective-permute-start.1 = (bf16[512,768]{1,0:T(8,128)(2,1)}, bf16[512,768]{1,0:T(8,128)(2,1)}, u32[]{:S(2)}, u32[]{:S(2)}) collective-permute-start(bf16[512,768]{1,0:T(8,128)(2,1)} %get-tuple-element.127), channel_id=1, source_target_pairs={{0,1},{1,0},{2,3},{3,2},{4,5},{5,4},{6,7},{7,6},{8,9},{9,8},{10,11... | collective-permute-start | bytes 2359304 | tf_op jit(solution)/shard_map/ppermute | solution.py:217
  591.0 21.1 %collective-permute-start.2 = (bf16[512,768]{1,0:T(8,128)(2,1)}, bf16[512,768]{1,0:T(8,128)(2,1)}, u32[]{:S(2)}, u32[]{:S(2)}) collective-permute-start(bf16[512,768]{1,0:T(8,128)(2,1)} %fusion.227), channel_id=1, source_target_pairs={{2,0},{3,1},{6,4},{7,5},{10,8},{11,9},{14,12},{15,13},{18,16},{19,... | collective-permute-start | bytes 2359304 | tf_op jit(solution)/shard_map/ppermute | solution.py:227
  594.9 232.3 %all-gather.33.cloned.1.call-start = ((), (), s32[]{:S(2)}) async-start(), calls=%async_computation.10 | async-start | bytes 7864320 | tf_op jit(solution)/shard_map/all_gather | solution.py:221
  682.5 2.7 collective-permute-start.9
  686.7 255.5 %all-gather.31.cloned.1.call-start = ((), (), s32[]{:S(2)}) async-start(), calls=%async_computation.9 | async-start | bytes 7864320 | tf_op jit(solution)/shard_map/all_gather | solution.py:221
  717.2 2.4 collective-permute-start.3
  721.0 384.2 %reduce-scatter.2.cloned.1.call-start = ((), (), s32[]{:S(2)}) async-start(), calls=%async_computation.4 | async-start | bytes 11919360 | tf_op jit(solution)/shard_map/reduce_scatter | solution.py:243
  728.0 48.6 %collective-permute-start.6 = (bf16[512,768]{1,0:T(8,128)(2,1)}, bf16[512,768]{1,0:T(8,128)(2,1)}, u32[]{:S(2)}, u32[]{:S(2)}) collective-permute-start(bf16[512,768]{1,0:T(8,128)(2,1)} %get-tuple-element.115), channel_id=1, source_target_pairs={{0,1},{1,0},{2,3},{3,2},{4,5},{5,4},{6,7},{7,6},{8,9},{9,8},{10,11... | collective-permute-start | bytes 2359304 | tf_op jit(solution)/shard_map/ppermute | solution.py:217
  734.1 55.2 %collective-permute-start.4 = (bf16[512,2304]{1,0:T(8,128)(2,1)}, bf16[512,2304]{1,0:T(8,128)(2,1)}, u32[]{:S(2)}, u32[]{:S(2)}) collective-permute-start(bf16[512,2304]{1,0:T(8,128)(2,1)} %get-tuple-element.108), channel_id=1, source_target_pairs={{0,1},{1,0},{2,3},{3,2},{4,5},{5,4},{6,7},{7,6},{8,9},{9,8},{10,11... | collective-permute-start | bytes 7077896 | tf_op jit(solution)/shard_map/ppermute | solution.py:217
  739.9 39.4 %collective-permute-start.5 = (bf16[512,768]{1,0:T(8,128)(2,1)}, bf16[512,768]{1,0:T(8,128)(2,1)S(1)}, u32[]{:S(2)}, u32[]{:S(2)}) collective-permute-start(bf16[512,768]{1,0:T(8,128)(2,1)} %get-tuple-element.105), channel_id=1, source_target_pairs={{0,1},{1,0},{2,3},{3,2},{4,5},{5,4},{6,7},{7,6},{8,9},{9,8},{10,11... | collective-permute-start | bytes 2359304 | tf_op jit(solution)/shard_map/ppermute | solution.py:217
  776.1 4.6 collective-permute-start.8
  776.3 7.1 collective-permute-start.7
  942.2 72.7 %collective-permute-start.10 = (bf16[4,2,512,768]{3,2,1,0:T(8,128)(2,1)}, bf16[4,2,512,768]{3,2,1,0:T(8,128)(2,1)}, u32[]{:S(2)}, u32[]{:S(2)}) collective-permute-start(bf16[4,2,512,768]{3,2,1,0:T(8,128)(2,1)} %bitcast.277), channel_id=1, source_target_pairs={{1,0},{2,1},{3,2},{5,4},{6,5},{7,6},{9,8},{10,9},{11,10},{13,12},{... | collective-permute-start | bytes 18874376 | tf_op jit(solution)/shard_map/ppermute | solution.py:230
  (143 other events, 3637.2 us)
Sparse Core Ops, SparseCore 0:
  10.8 79.8 all-gather.16
  93.2 79.1 all-gather.20
  175.2 77.1 all-gather.24
  254.4 22.6 all-gather.18
  278.5 23.7 all-gather.22
  303.7 23.7 all-gather.26
  595.0 117.1 all-gather.28
  713.7 113.3 all-gather.32
  828.7 113.3 all-gather.30
  944.4 160.7 reduce-scatter.1

commit v2 on v1

--- a/solution.py
+++ b/solution.py
@@ -1,14 +1,14 @@
-import functools
-
 import jax
 import jax.numpy as jnp
 from jax import lax
 from jax.experimental import pallas as pl
 from jax.experimental.pallas import tpu as pltpu
+from jax.experimental.layout import Layout, with_layout_constraint
 from jax.sharding import Mesh, PartitionSpec as P
 
 LN_EPS = 1e-5
 MASK_VALUE = -1e9
+ROW_MAJOR = Layout((0, 1))
 F32 = jnp.float32
 BF16 = jnp.bfloat16
 NT = (((1,), (1,)), ((), ()))
@@ -113,12 +113,10 @@
     return d_v, jnp.sum(d_out * xhat, axis=0), jnp.sum(d_out, axis=0)
 
 
-def gelu(value):
-    return jax.nn.gelu(value, approximate=False)
-
-
-def gelu_back(up, d_hidden_bf):
-    return jax.vjp(gelu, up)[1](d_hidden_bf.astype(F32))[0]
+def gelu_pair(up):
+    cdf = 0.5 * (1.0 + lax.erf(up * (0.5 ** 0.5)))
+    slope = cdf + up * (jnp.exp(-0.5 * up * up) * ((2.0 * jnp.pi) ** -0.5))
+    return (up * cdf).astype(BF16), slope
 
 
 def layer_forward(h_in, params, length):
@@ -130,17 +128,17 @@
     mid = (h_in.astype(F32) + dot(context, w_att[n_qkv:], NN) + vec[2]).astype(BF16)
     normed2 = layer_norm(mid, vec[3], vec[4])
     up = dot(normed2, w_up, NT) + b_up
-    hidden = gelu(up).astype(BF16)
+    hidden, slope = gelu_pair(up)
     out = (mid.astype(F32) + dot(hidden, w_down, NN) + vec[5]).astype(BF16)
-    return out, (h_in, normed, qkv, context, mid, up)
+    return out, (h_in, normed, qkv, context, mid, slope)
 
 
 def layer_backward(g_out, saved, params, length):
-    w_att, w_up, w_down, vec, b_qkv, b_up = params
+    w_att, w_up, w_down, vec, b_qkv, _ = params
     n_qkv = b_qkv.shape[0]
-    h_in, normed, qkv, context, mid, up = saved
+    h_in, normed, qkv, context, mid, slope = saved
     d_hidden = dot(g_out, w_down, NT).astype(BF16)
-    d_up = gelu_back(up, d_hidden).astype(BF16)
+    d_up = (d_hidden.astype(F32) * slope).astype(BF16)
     d_normed2 = dot(d_up, w_up, NN).astype(BF16)
     d_mid, d_gain2, d_bias2 = norm_back(mid, vec[3], d_normed2, g_out)
     d_context = dot(d_mid, w_att[n_qkv:], NT).astype(BF16)
@@ -164,32 +162,58 @@
     stage_spec = P(pp, 'dp', None, None, None)
     swap = [(0, 1), (1, 0)]
 
-    def body(x_in, seq_len, dy_out, *weights):
+    def compute(x_in, seq_len, dy_out, *weights):
         (ln1_gain, ln1_bias, w_qkv, b_qkv, w_attn, b_attn, ln2_gain, ln2_bias, w_up, b_up, w_down, b_down) = tuple(weight[0] for weight in weights)
         dp_id, tp_id, py_id, core_id = (lax.axis_index(name) for name in ('dp', 'tp', 'py', 'core'))
-        n_micro, _, rows, width = x_in.shape
+        _, _, rows, width = x_in.shape
         n_local = w_attn.shape[0] * w_attn.shape[1]
         first_core, first_pair = core_id == 0, py_id == 0
 
-        def gather_weight(shard):
-            half = shard.shape[0] // n_dp
-            piece = lax.dynamic_slice_in_dim(shard, dp_id * half, half, 0)
-            return lax.all_gather(piece, ('tp', 'dp'), axis=0, tiled=True)
-
-        att_shard = jnp.concatenate([w_qkv.reshape(3, width, n_local).transpose(0, 2, 1).reshape(3 * n_local, width), w_attn.reshape(n_local, width)])
-        att_full = gather_weight(att_shard).reshape(n_tp, 4, n_local, width).transpose(1, 0, 2, 3).reshape(4 * n_tp * n_local, width)
-        up_full = gather_weight(w_up.T)
-        down_full = gather_weight(w_down)
-        both = [lax.all_gather(full, 'core', axis=0) for full in (att_full, up_full, down_full)]
-
-        b_qkv_flat = b_qkv.reshape(3 * n_local)
-        packed = jnp.concatenate([jnp.stack([ln1_gain, ln1_bias, b_attn, ln2_gain, ln2_bias, b_down]), jnp.pad(b_qkv_flat, (0, width - 3 * n_local))[None], b_up.reshape(-1, width)])
-        packed = lax.all_gather(packed, ('core', 'tp'), axis=0).reshape(2, n_tp, -1, width)
+        def by_core(on_first, on_second):
+            return jnp.where(first_core, on_first, on_second)
+
+        def gather_tp(value):
+            return lax.all_gather(value, 'tp', axis=0)
+
+        def core_swap(value):
+            return lax.ppermute(value, 'core', swap)
+
+        b_qkv_row = jnp.pad(b_qkv.reshape(1, -1), ((0, 0), (0, width - 3 * n_local)))
+        packed = jnp.concatenate([jnp.stack([ln1_gain, ln1_bias, b_attn, ln2_gain, ln2_bias, b_down]), b_qkv_row, b_up.reshape(-1, width)])
+        packed = gather_tp(packed)
+        packed_other = core_swap(packed)
+        packed = (by_core(packed, packed_other), by_core(packed_other, packed))
+
+        att_shard = jnp.concatenate([w_qkv.reshape(3, width, n_local).transpose(0, 2, 1), w_attn.reshape(1, n_local, width)])
+        shards = [att_shard, w_up.T.reshape(4, -1, width), w_down.reshape(4, -1, width)]
+        pieces = ([], [])
+        for shard in shards:
+            mine = lax.dynamic_index_in_dim(shard, 2 * dp_id + core_id, 0, keepdims=False)
+            theirs = lax.dynamic_index_in_dim(shard, 2 * dp_id + 1 - core_id, 0, keepdims=False)
+            mine, theirs = with_layout_constraint(mine, ROW_MAJOR), with_layout_constraint(theirs, ROW_MAJOR)
+            got = core_swap(theirs)
+            pieces[0].append(by_core(mine, got))
+            pieces[1].append(by_core(got, mine))
+
+        gathered = [gather_tp(piece) for piece in pieces[0] + pieces[1]]
+        from_x = []
+        for own_x in gathered:
+            from_x.append(lax.ppermute(own_x, 'dp', swap))
+
+        def assemble(i):
+            own_x, other_x = gathered[i], from_x[i]
+            own_swapped = core_swap(own_x)
+            full = jnp.zeros((4,) + own_x.shape, BF16)
+            for row, x_pos, c_pos in ((own_swapped, dp_id, 1 - core_id), (own_x, dp_id, core_id), (other_x, 1 - dp_id, core_id), (core_swap(other_x), 1 - dp_id, 1 - core_id)):
+                row, slot = lax.optimization_barrier((row, 2 * x_pos + c_pos))
+                full = lax.dynamic_update_index_in_dim(full, row, slot, 0)
+            return full.reshape(-1, width)
 
         def layer_params(layer):
-            b_qkv_full = packed[layer, :, 6, :3 * n_local].reshape(n_tp, 3, n_local).transpose(1, 0, 2).reshape(-1)
-            b_up_full = packed[layer, :, 7:].reshape(-1)
-            return tuple(arr[layer] for arr in both) + (packed[layer, 0, :6], b_qkv_full, b_up_full)
+            w_att, w_upt, w_dn = (assemble(i) for i in range(3 * layer, 3 * layer + 3))
+            b_qkv_full = packed[layer][:, 6, :3 * n_local].reshape(n_tp, 3, n_local).transpose(1, 0, 2).reshape(-1)
+            b_up_full = packed[layer][:, 7:].reshape(n_tp, 4, -1).transpose(1, 0, 2).reshape(-1)
+            return (w_att, w_upt, w_dn, packed[layer][0, :6], b_qkv_full, b_up_full)
 
         params = (layer_params(0), layer_params(1))
 
@@ -203,54 +227,65 @@
             out, saved1 = layer_forward(mid, params[1], length)
             return (mid, out), (saved0, saved1)
 
-        def backward(g, saved):
-            dx1, keep1 = layer_backward(g, saved[1], params[1], length)
-            dx0, keep0 = layer_backward(dx1, saved[0], params[0], length)
-            return (dx0, dx1), (keep0, keep1)
+        def pair_pick(phase_a, phase_b):
+            return jnp.where(first_pair, phase_a, phase_b)
 
         outs_a, saved_a = forward(my_sequence(x_in))
         outs_b, saved_b = forward(lax.ppermute(outs_a[1], 'py', [(0, 1)]))
 
-        def own_stage(phase0, phase1):
-            by_layer = [jnp.where(first_pair, phase0[layer], phase1[layer]) for layer in range(2)]
-            keep = jnp.where(first_core, by_layer[0], by_layer[1])
-            other = lax.ppermute(jnp.where(first_core, by_layer[1], by_layer[0]), 'core', swap)
-            return jnp.stack([jnp.where(first_core, keep, other), jnp.where(first_core, other, keep)])
-
-        def gather_tokens(phase0, phase1):
-            return lax.all_gather(own_stage(phase0, phase1), 'tp', axis=0)
-
-        stage_out = gather_tokens(outs_a, outs_b)
-        mid_all = gather_tokens([saved[4] for saved in saved_a], [saved[4] for saved in saved_b])
-
-        dxs_b, keeps_b = backward(my_sequence(dy_out), saved_b)
-        dxs_a, keeps_a = backward(lax.ppermute(dxs_b[0], 'py', [(1, 0)]), saved_a)
-
-        stage_dx = gather_tokens(dxs_a, dxs_b)
-        next_dx = lax.ppermute(stage_dx, pp, [(s + 1, s) for s in range(n_pp - 1)])
-        is_last = (~first_pair) & (~first_core)
-        g_all = jnp.where(is_last, dy_out, next_dx).reshape(-1, width)
-
-        d_qkv, d_mid, context, normed, small = (own_stage([keep[i] for keep in keeps_a], [keep[i] for keep in keeps_b]) for i in range(5))
-        tokens = 2 * rows
-        gw_qkv = dot(d_qkv.reshape(tokens, -1), normed.reshape(tokens, -1), TN)
-        gw_attn = dot(context.reshape(tokens, -1), d_mid.reshape(tokens, -1), TN)
-        small = small[0] + small[1]
-        gw_att = jnp.concatenate([gw_qkv, gw_attn]).reshape(4, n_tp, n_local, width).transpose(1, 0, 2, 3).reshape(n_tp, 4 * n_local, width)
-        gb_qkv = small[5:].reshape(3, n_tp, n_local).transpose(1, 0, 2).reshape(n_tp, 1, 3 * n_local)
-        gb_qkv = jnp.pad(gb_qkv, ((0, 0), (0, 2), (0, width - 3 * n_local)))
-        payload = jnp.concatenate([gw_att, jnp.broadcast_to(small[None, :5], (n_tp, 5, width)), gb_qkv], axis=1)
-        reduced = lax.psum_scatter(payload, 'tp', scatter_dimension=0, tiled=False)
-        g_qkv = reduced[:3 * n_local].reshape(3, n_local, width).transpose(0, 2, 1).reshape(w_qkv.shape)
-        g_attn = reduced[3 * n_local:4 * n_local].reshape(w_attn.shape)
-        g_vec = reduced[4 * n_local:]
-
-        mid_flat = mid_all.reshape(-1, width)
-        normed2 = layer_norm(mid_flat, ln2_gain, ln2_bias)
-        up = dot(normed2, w_up, NN) + b_up
-        hidden = gelu(up).astype(BF16)
-        d_hidden = dot(g_all, w_down, NT).astype(BF16)
-        d_up = gelu_back(up, d_hidden)
+        def own_stage(phase_a, phase_b):
+            layers = [pair_pick(phase_a[layer], phase_b[layer]) for layer in range(2)]
+            keep, other = by_core(*layers), core_swap(by_core(layers[1], layers[0]))
+            return jnp.stack([by_core(keep, other), by_core(other, keep)])
+
+        own_out = own_stage(outs_a, outs_b)
+        own_mid = own_stage([saved[4] for saved in saved_a], [saved[4] for saved in saved_b])
+        g_top, own_out, own_mid = lax.optimization_barrier((my_sequence(dy_out), own_out, own_mid))
+        stage_out = gather_tp(own_out)
+        mid_all = gather_tp(own_mid)
+
+        def weight_payload(keep_a, keep_b):
+            d_qkv_a, d_qkv_b = keep_a[0], keep_b[0]
+            d_q, d_k, d_v = (pair_pick(d_qkv_a[:, i * width:(i + 1) * width], d_qkv_b[:, i * width:(i + 1) * width]) for i in range(3))
+            d_mid, context, normed, small = (pair_pick(keep_a[i], keep_b[i]) for i in range(1, 5))
+            got = core_swap(jnp.stack([by_core(d_v, d_q), by_core(context, d_k), normed, d_mid]))
+            left0, left1 = by_core(d_q, d_v), by_core(d_k, context)
+            right1 = by_core(normed, d_mid)
+            grad0 = dot(left0, normed, TN) + dot(got[0], got[2], TN)
+            grad1 = dot(left1, right1, TN) + dot(got[1], by_core(got[2], got[3]), TN)
+            b_rows = small[5:].reshape(3, n_tp, n_local).transpose(1, 0, 2).reshape(n_tp, 1, 3 * n_local)
+            b_rows = jnp.pad(b_rows, ((0, 0), (0, 2), (0, width - 3 * n_local)))
+            return jnp.concatenate([grad0.reshape(n_tp, n_local, width), grad1.reshape(n_tp, n_local, width), jnp.broadcast_to(small[None, :5], (n_tp, 5, width)), b_rows], axis=1)
+
+        def both_rows(gathered):
+            other = core_swap(gathered)
+            return jnp.stack([by_core(gathered, other), by_core(other, gathered)], axis=1)
+
+        dx1_b, keep1_b = layer_backward(g_top, saved_b[1], params[1], length)
+        dx0_b, keep0_b = layer_backward(dx1_b, saved_b[0], params[0], length)
+        dx1_a, keep1_a = layer_backward(lax.ppermute(dx0_b, 'py', [(1, 0)]), saved_a[1], params[1], length)
+        own_dx1, dx1_a, keep1_a = lax.optimization_barrier((pair_pick(dx1_a, dx1_b), dx1_a, keep1_a))
+        dx1_all = both_rows(gather_tp(own_dx1))
+        dx0_a, keep0_a = layer_backward(dx1_a, saved_a[0], params[0], length)
+        own_dx0, payload1 = lax.optimization_barrier((pair_pick(dx0_a, dx0_b), weight_payload(keep1_a, keep1_b)))
+        dx0_all = both_rows(gather_tp(own_dx0))
+        reduced1 = lax.psum_scatter(payload1, 'tp', scatter_dimension=0, tiled=False)
+        reduced0 = lax.psum_scatter(weight_payload(keep0_a, keep0_b), 'tp', scatter_dimension=0, tiled=False)
+
+        stage_dx = by_core(dx0_all, dx1_all)
+        from_next = lax.ppermute(dx0_all, pp, [(2, 1)])
+        g_all = by_core(dx1_all, pair_pick(from_next, dy_out)).reshape(-1, width)
+
+        reduced = by_core(reduced0, reduced1)
+        reduced_other = core_swap(by_core(reduced1, reduced0))
+        halves = by_core(reduced, reduced_other), by_core(reduced_other, reduced)
+        g_qkv = jnp.concatenate([halves[0][:2 * n_local], halves[1][:n_local]]).reshape(3, n_local, width).transpose(0, 2, 1).reshape(w_qkv.shape)
+        g_attn = halves[1][n_local:2 * n_local].reshape(w_attn.shape)
+        g_vec = halves[0][2 * n_local:] + halves[1][2 * n_local:]
+
+        normed2 = layer_norm(mid_all.reshape(-1, width), ln2_gain, ln2_bias)
+        hidden, slope = gelu_pair(dot(normed2, w_up, NN) + b_up)
+        d_up = dot(g_all, w_down, NT).astype(BF16).astype(F32) * slope
         g_w_up = dot(normed2, d_up.astype(BF16), TN)
         g_w_down = dot(hidden, g_all, TN)
         g_b_up = jnp.sum(d_up, axis=0)
@@ -259,4 +294,4 @@
         grads = (g_vec[0], g_vec[1], g_qkv, g_vec[5, :3 * n_local].reshape(b_qkv.shape), g_attn, g_vec[2], g_vec[3], g_vec[4], g_w_up, g_b_up, g_w_down, g_b_down)
         return (stage_out[None], stage_dx[None]) + tuple(grad[None] for grad in grads)
 
-    return jax.shard_map(body, mesh=split, in_specs=(act_spec, P('dp', None), act_spec) + param_specs, out_specs=(stage_spec, stage_spec) + grad_specs, check_vma=False)
+    return jax.shard_map(compute, mesh=split, in_specs=(act_spec, P('dp', None), act_spec) + param_specs, out_specs=(stage_spec, stage_spec) + grad_specs, check_vma=False)

time: 1140 us -> 1290 us (1.13)
  waiting for transfers between devices: 458 us -> 664 us
  matrix products: 321 us -> 217 us
  local copies, waits for them, and re-layouts: 69.9 us -> 103 us
  starting transfers between devices: 11.7 us -> 41.6 us
  blocking collectives: 25.1 us -> 10.3 us
    reduce_scatter x1 -> x2, waiting for transfers between devices: 40.3 us -> 151 us  [the longest x1 90.3 us: compute(): lax.psum_scatter(payload1, 'tp', scatter_dimension=0, tiled=False)]
    dot_general x38 -> x40, matrix products: 321 us -> 217 us  [dot(): return lax.dot_general(lhs, rhs, dims, preferred_element_type=F32)]
    all_gather x9 -> x10, waiting for transfers between devices: 358 us -> 427 us  [gather_tp(): return lax.all_gather(value, 'tp', axis=0)]
    dynamic_update_slice x0 -> x24, local copies, waits for them, and re-layouts: none -> 48.4 us  [assemble(): full = lax.dynamic_update_index_in_dim(full, row, slot, 0)]
    ppermute x11 -> x32, starting transfers between devices: 11.2 us -> 40.8 us  [the longest x23 28.7 us: core_swap(): return lax.ppermute(value, 'core', swap)]
    ppermute x11 -> x32, waiting for transfers between devices: 59.4 us -> 82.8 us  [the longest x6 42.5 us: compute(): from_x.append(lax.ppermute(own_x, 'dp', swap))]
    another operation x20, local copies, waits for them, and re-layouts: 20.7 us -> 0.08 us  [layer_backward(): jnp.stack([d_gain1, d_bias1, d_b_attn, d_gain2, d_bias2])]
    another operation x4 -> x10, local copies, waits for them, and re-layouts: 0.92 us -> 16.7 us  [the longest x1 0.67 us: body(): grad[None]]
  transfers between devices with their start and end apart: 21 -> 44, of which waited for: 12 -> 20; matrix products, arithmetic and copies ran while one was open for 30% -> 16% of each run, Pallas kernels for 6% -> 1%
where the time goes in v2:
time: 1290 us; the launch traced here: 1280 us
  waiting for transfers between devices  664 us (51%)
  matrix products  217 us (17%)
  Pallas kernels  129 us (10%)
  local copies, waits for them, and re-layouts  103 us (8%)
  other arithmetic  102 us (8%)
  starting transfers between devices  41.6 us (3%)
  between operations  16.6 us (1%)
    all_gather x10, waiting for transfers between devices, gather_tp(): return lax.all_gather(value, 'tp', axis=0)  427 us
    dot_general x40, matrix products, dot(): return lax.dot_general(lhs, rhs, dims, preferred_element_type=F32)  217 us
    reduce_scatter x1, waiting for transfers between devices, compute(): lax.psum_scatter(payload1, 'tp', scatter_dimension=0, tiled=False)  90.3 us
    pallas_call x4, Pallas kernels, attn_bwd(): pl.pallas_call(attn_bwd_kernel, grid=(pairs,), out_shape=jax.ShapeDtypeSt...  76.7 us
    reduce_scatter x1, waiting for transfers between devices, compute(): lax.psum_scatter(weight_payload(keep0_a, keep0_b), 'tp', scatter_dimensio...  60.3 us
    pallas_call x4, Pallas kernels, attn_fwd(): pl.pallas_call(attn_fwd_kernel, grid=(pairs,), out_shape=jax.ShapeDtypeSt...  52.7 us
    dynamic_update_slice x24, local copies, waits for them, and re-layouts, assemble(): full = lax.dynamic_update_index_in_dim(full, row, slot, 0)  48.4 us
    ppermute x6, waiting for transfers between devices, compute(): from_x.append(lax.ppermute(own_x, 'dp', swap))  42.5 us
  transfers between devices with their start and end apart: 44, of which 20 were waited for; matrix products, arithmetic and copies ran while one was open for 16% of the time, Pallas kernels for 1%

profile of v2, /device:TPU:1, one launch (start us, length us, event | category | flops | bytes accessed | tf_op | source)
XLA Modules:
  0.0 1283.6 jit_solution(9542183636048207280)
XLA Ops:
  19.9 24.2 %all-gather.22.cloned.1.call-done = bf16[768,768]{1,0:T(8,128)(2,1)} async-done(((bf16[192,768]{1,0:T(8,128)(2,1)}), bf16[768,768]{1,0:T(8,128)(2,1)}) %all-gather.22.cloned.1.call-update) | async-done | bytes 1179664 | tf_op jit(solution)/shard_map/all_gather | solution.py:176
  82.4 25.4 %all-gather.26.cloned.1.call-done = bf16[768,768]{1,0:T(8,128)(2,1)} async-done(((bf16[192,768]{1,0:T(8,128)(2,1)}), bf16[768,768]{1,0:T(8,128)(2,1)}) %all-gather.26.cloned.1.call-update) | async-done | bytes 1179664 | tf_op jit(solution)/shard_map/all_gather | solution.py:176
  109.1 30.2 %all-gather.28.cloned.1.call-done = bf16[768,768]{1,0:T(8,128)(2,1)} async-done(((bf16[192,768]{1,0:T(8,128)(2,1)}), bf16[768,768]{1,0:T(8,128)(2,1)}) %all-gather.28.cloned.1.call-update) | async-done | bytes 1179664 | tf_op jit(solution)/shard_map/all_gather | solution.py:176
  139.3 31.5 %all-gather.30.cloned.1.call-done = bf16[768,768]{1,0:T(8,128)(2,1)} async-done(((bf16[192,768]{1,0:T(8,128)(2,1)}), bf16[768,768]{1,0:T(8,128)(2,1)}) %all-gather.30.cloned.1.call-update) | async-done | bytes 1179664 | tf_op jit(solution)/shard_map/all_gather | solution.py:176
  170.9 31.5 %all-gather.32.cloned.1.call-done = bf16[768,768]{1,0:T(8,128)(2,1)} async-done(((bf16[192,768]{1,0:T(8,128)(2,1)}), bf16[768,768]{1,0:T(8,128)(2,1)}) %all-gather.32.cloned.1.call-update) | async-done | bytes 1179664 | tf_op jit(solution)/shard_map/all_gather | solution.py:176
  259.2 20.3 %collective-permute-done.17 = bf16[4,192,768]{2,1,0:T(8,128)(2,1)} collective-permute-done((bf16[4,192,768]{2,1,0:T(8,128)(2,1)S(1)}, bf16[4,192,768]{2,1,0:T(8,128)(2,1)}, u32[]{:S(2)}, u32[]{:S(2)}) %collective-permute-start.17) | collective-permute-done | bytes 1179680 | tf_op jit(solution)/shard_map/ppermute | solution.py:201
  336.9 13.5 %attn_fwd.4 = bf16[512,768]{1,0:T(8,128)(2,1)} custom-call(s32[1]{0:T(128)} %bitcast.2.len_ref, bf16[512,2304]{1,0:T(8,128)(2,1)} %fusion.37.q_ref.k_ref.v_ref, bf16[512,2304]{1,0:T(8,128)(2,1)} %fusion.37.q_ref.k_ref.v_ref, bf16[512,2304]{1,0:T(8,128)(2,1)} %fusion.37.q_ref.k_ref.v_ref), custom_call_target="tpu_custom_call" | custom-call | flops 3221225472 | bytes 3145728 | tf_op jit(solution)/shard_map/attn_fwd/pallas_call | solution.py:71
  375.6 13.1 %attn_fwd.5 = bf16[512,768]{1,0:T(8,128)(2,1)} custom-call(s32[1]{0:T(128)} %bitcast.2.len_ref, bf16[512,2304]{1,0:T(8,128)(2,1)} %fusion.38.q_ref.k_ref.v_ref, bf16[512,2304]{1,0:T(8,128)(2,1)} %fusion.38.q_ref.k_ref.v_ref, bf16[512,2304]{1,0:T(8,128)(2,1)} %fusion.38.q_ref.k_ref.v_ref), custom_call_target="tpu_custom_call" | custom-call | flops 3221225472 | bytes 3145728 | tf_op jit(solution)/shard_map/attn_fwd/pallas_call | solution.py:71
  396.4 16.9 %fusion.219 = f32[512,3072]{1,0:T(8,128)S(1)} fusion(bf16[3072,768]{1,0:T(8,128)(2,1)} %bitcast.54, bf16[512,768]{1,0:T(8,128)(2,1)S(1)} %get-tuple-element.281, f32[768]{0:T(1024)S(1)} %copy-done.85, f32[768]{0:T(1024)S(1)} %get-tuple-element.210, f32[512]{0:T(512)S(1)} %add_rsqrt_fusion.5, f32[512]{0:T(512)S(1)} %broadcast_multiply_fusion.21), kind=kOutput, calls=%fused_computation.364 | convolution fusion | flops 2418278400 | bytes 11806720 | tf_op jit(solution)/shard_map/dot_general | solution.py:20
  424.3 16.4 %collective-permute-done.22 = bf16[512,768]{1,0:T(8,128)(2,1)S(1)} collective-permute-done((bf16[512,768]{1,0:T(8,128)(2,1)S(1)}, bf16[512,768]{1,0:T(8,128)(2,1)S(1)}, u32[]{:S(2)}, u32[]{:S(2)}) %collective-permute-start.22) | collective-permute-done | bytes 786464 | tf_op jit(solution)/shard_map/ppermute | solution.py:234
  446.9 13.1 %attn_fwd.6 = bf16[512,768]{1,0:T(8,128)(2,1)} custom-call(s32[1]{0:T(128)} %bitcast.2.len_ref, bf16[512,2304]{1,0:T(8,128)(2,1)} %fusion.39.q_ref.k_ref.v_ref, bf16[512,2304]{1,0:T(8,128)(2,1)} %fusion.39.q_ref.k_ref.v_ref, bf16[512,2304]{1,0:T(8,128)(2,1)} %fusion.39.q_ref.k_ref.v_ref), custom_call_target="tpu_custom_call" | custom-call | flops 3221225472 | bytes 3145728 | tf_op jit(solution)/shard_map/attn_fwd/pallas_call | solution.py:71
  479.4 13.1 %attn_fwd.7 = bf16[512,768]{1,0:T(8,128)(2,1)} custom-call(s32[1]{0:T(128)} %bitcast.2.len_ref, bf16[512,2304]{1,0:T(8,128)(2,1)} %fusion.40.q_ref.k_ref.v_ref, bf16[512,2304]{1,0:T(8,128)(2,1)} %fusion.40.q_ref.k_ref.v_ref, bf16[512,2304]{1,0:T(8,128)(2,1)} %fusion.40.q_ref.k_ref.v_ref), custom_call_target="tpu_custom_call" | custom-call | flops 3221225472 | bytes 3145728 | tf_op jit(solution)/shard_map/attn_fwd/pallas_call | solution.py:71
  532.6 19.1 %attn_bwd.4 = bf16[512,2304]{1,0:T(8,128)(2,1)} custom-call(s32[1]{0:T(128)} %bitcast.2.len_ref, bf16[512,2304]{1,0:T(8,128)(2,1)} %fusion.40.q_ref.k_ref.v_ref, bf16[512,2304]{1,0:T(8,128)(2,1)} %fusion.40.q_ref.k_ref.v_ref, bf16[512,2304]{1,0:T(8,128)(2,1)} %fusion.40.q_ref.k_ref.v_ref, bf16[512,768]{1,0:T(8,128)(2,1)} %convolution_convert_fusion.8.dctx_ref), custom_call_target="tpu_custom_call" | custom-call | flops 8053063680 | bytes 5505024 | tf_op jit(solution)/shard_map/attn_bwd/pallas_call | solution.py:85
  573.1 19.2 %attn_bwd.5 = bf16[512,2304]{1,0:T(8,128)(2,1)} custom-call(s32[1]{0:T(128)} %bitcast.2.len_ref, bf16[512,2304]{1,0:T(8,128)(2,1)} %fusion.39.q_ref.k_ref.v_ref, bf16[512,2304]{1,0:T(8,128)(2,1)} %fusion.39.q_ref.k_ref.v_ref, bf16[512,2304]{1,0:T(8,128)(2,1)} %fusion.39.q_ref.k_ref.v_ref, bf16[512,768]{1,0:T(8,128)(2,1)} %convolution_convert_fusion.7.dctx_ref), custom_call_target="tpu_custom_call" | custom-call | flops 8053063680 | bytes 5505024 | tf_op jit(solution)/shard_map/attn_bwd/pallas_call | solution.py:85
  600.9 19.4 %collective-permute-done.25 = bf16[512,768]{1,0:T(8,128)(2,1)} collective-permute-done((bf16[512,768]{1,0:T(8,128)(2,1)}, bf16[512,768]{1,0:T(8,128)(2,1)}, u32[]{:S(2)}, u32[]{:S(2)}) %collective-permute-start.25) | collective-permute-done | bytes 786464 | tf_op jit(solution)/shard_map/ppermute | solution.py:266
  620.3 12.4 fusion.195
  637.8 19.4 %attn_bwd.6 = bf16[512,2304]{1,0:T(8,128)(2,1)} custom-call(s32[1]{0:T(128)} %bitcast.2.len_ref, bf16[512,2304]{1,0:T(8,128)(2,1)} %fusion.38.q_ref.k_ref.v_ref, bf16[512,2304]{1,0:T(8,128)(2,1)} %fusion.38.q_ref.k_ref.v_ref, bf16[512,2304]{1,0:T(8,128)(2,1)} %fusion.38.q_ref.k_ref.v_ref, bf16[512,768]{1,0:T(8,128)(2,1)} %convolution_convert_fusion.6.dctx_ref), custom_call_target="tpu_custom_call" | custom-call | flops 8053063680 | bytes 5505024 | tf_op jit(solution)/shard_map/attn_bwd/pallas_call | solution.py:85
  673.5 12.3 fusion.197
  692.4 19.0 %attn_bwd.7 = bf16[512,2304]{1,0:T(8,128)(2,1)} custom-call(s32[1]{0:T(128)} %bitcast.2.len_ref, bf16[512,2304]{1,0:T(8,128)(2,1)} %fusion.37.q_ref.k_ref.v_ref, bf16[512,2304]{1,0:T(8,128)(2,1)} %fusion.37.q_ref.k_ref.v_ref, bf16[512,2304]{1,0:T(8,128)(2,1)} %fusion.37.q_ref.k_ref.v_ref, bf16[512,768]{1,0:T(8,128)(2,1)} %convolution_convert_fusion.5.dctx_ref), custom_call_target="tpu_custom_call" | custom-call | flops 8053063680 | bytes 5505024 | tf_op jit(solution)/shard_map/attn_bwd/pallas_call | solution.py:85
  754.1 57.5 %all-gather.36.cloned.1.call-done = bf16[2048,768]{1,0:T(8,128)(2,1)} async-done(((bf16[512,768]{1,0:T(8,128)(2,1)}), bf16[2048,768]{1,0:T(8,128)(2,1)}) %all-gather.36.cloned.1.call-update) | async-done | bytes 3145744 | tf_op jit(solution)/shard_map/all_gather | solution.py:176
  818.4 109.1 %all-gather.40.cloned.1.call-done = bf16[8,512,768]{2,1,0:T(8,128)(2,1)} async-done(((bf16[2,512,768]{2,1,0:T(8,128)(2,1)}), bf16[8,512,768]{2,1,0:T(8,128)(2,1)}) %all-gather.40.cloned.1.call-update) | async-done | bytes 6291472 | tf_op jit(solution)/shard_map/all_gather | solution.py:176
  954.8 60.3 %reduce-scatter.3.cloned.1.call-done = f32[1,392,768]{2,1,0:T(8,128)} async-done(((f32[4,392,768]{2,1,0:T(8,128)}), f32[1,392,768]{2,1,0:T(8,128)}) %reduce-scatter.3.cloned.1.call-update) | async-done | bytes 1204240 | tf_op jit(solution)/shard_map/reduce_scatter | solution.py:273
  1015.1 90.3 %reduce-scatter.5.cloned.1.call-done = f32[1,392,768]{2,1,0:T(8,128)} async-done(((f32[4,392,768]{2,1,0:T(8,128)}), f32[1,392,768]{2,1,0:T(8,128)}) %reduce-scatter.5.cloned.1.call-update) | async-done | bytes 1204240 | tf_op jit(solution)/shard_map/reduce_scatter | solution.py:272
  1115.6 107.9 %all-gather.34.cloned.1.call-done = bf16[8,512,768]{2,1,0:T(8,128)(2,1)} async-done(((bf16[2,512,768]{2,1,0:T(8,128)(2,1)}), bf16[8,512,768]{2,1,0:T(8,128)(2,1)}) %all-gather.34.cloned.1.call-update) | async-done | bytes 6291472 | tf_op jit(solution)/shard_map/all_gather | solution.py:176
  (548 shorter events, 471.9 us)
Async XLA Ops:
  12.2 63.9 %all-gather.24.cloned.1.call-start = ((), (), s32[]{:S(2)}) async-start(), calls=%async_computation.5 | async-start | bytes 1474560 | tf_op jit(solution)/shard_map/all_gather | solution.py:176
  15.5 92.3 %all-gather.26.cloned.1.call-start = ((), (), s32[]{:S(2)}) async-start(), calls=%async_computation.6 | async-start | bytes 1474560 | tf_op jit(solution)/shard_map/all_gather | solution.py:176
  18.1 121.2 %all-gather.28.cloned.1.call-start = ((), (), s32[]{:S(2)}) async-start(), calls=%async_computation.7 | async-start | bytes 1474560 | tf_op jit(solution)/shard_map/all_gather | solution.py:176
  18.7 152.1 %all-gather.30.cloned.1.call-start = ((), (), s32[]{:S(2)}) async-start(), calls=%async_computation.8 | async-start | bytes 1474560 | tf_op jit(solution)/shard_map/all_gather | solution.py:176
  19.3 183.1 %all-gather.32.cloned.1.call-start = ((), (), s32[]{:S(2)}) async-start(), calls=%async_computation.9 | async-start | bytes 1474560 | tf_op jit(solution)/shard_map/all_gather | solution.py:176
  19.9 733.4 %all-gather.38.cloned.1.call-start = ((), (), s32[]{:S(2)}) async-start(), calls=%async_computation.12 | async-start | bytes 3932160 | tf_op jit(solution)/shard_map/all_gather | solution.py:176
  44.1 158.3 %collective-permute-start.2 = (bf16[4,192,768]{2,1,0:T(8,128)(2,1)}, bf16[4,192,768]{2,1,0:T(8,128)(2,1)S(1)}, u32[]{:S(2)}, u32[]{:S(2)}) collective-permute-start(bf16[4,192,768]{2,1,0:T(8,128)(2,1)} %bitcast.383), channel_id=1, source_target_pairs={{0,1},{1,0},{2,3},{3,2},{4,5},{5,4},{6,7},{7,6},{8,9},{9,8},{10,11... | collective-permute-start | bytes 3538952 | tf_op jit(solution)/shard_map/ppermute | solution.py:179
  62.1 146.9 %collective-permute-start.3 = (bf16[4,192,768]{2,1,0:T(8,128)(2,1)}, bf16[4,192,768]{2,1,0:T(8,128)(2,1)}, u32[]{:S(2)}, u32[]{:S(2)}) collective-permute-start(bf16[4,192,768]{2,1,0:T(8,128)(2,1)} %bitcast.384), channel_id=1, source_target_pairs={{0,16},{16,0},{1,17},{17,1},{2,18},{18,2},{3,19},{19,3},{4,20},{20... | collective-permute-start | bytes 3538952 | tf_op jit(solution)/shard_map/ppermute | solution.py:201
  76.1 136.8 %collective-permute-start.6 = (bf16[4,192,768]{2,1,0:T(8,128)(2,1)}, bf16[4,192,768]{2,1,0:T(8,128)(2,1)}, u32[]{:S(2)}, u32[]{:S(2)}) collective-permute-start(bf16[4,192,768]{2,1,0:T(8,128)(2,1)} %bitcast.380), channel_id=1, source_target_pairs={{0,1},{1,0},{2,3},{3,2},{4,5},{5,4},{6,7},{7,6},{8,9},{9,8},{10,11... | collective-permute-start | bytes 3538952 | tf_op jit(solution)/shard_map/ppermute | solution.py:179
  77.3 135.9 %collective-permute-start.7 = (bf16[4,192,768]{2,1,0:T(8,128)(2,1)}, bf16[4,192,768]{2,1,0:T(8,128)(2,1)S(1)}, u32[]{:S(2)}, u32[]{:S(2)}) collective-permute-start(bf16[4,192,768]{2,1,0:T(8,128)(2,1)} %bitcast.381), channel_id=1, source_target_pairs={{0,16},{16,0},{1,17},{17,1},{2,18},{18,2},{3,19},{19,3},{4,20},{20... | collective-permute-start | bytes 3538952 | tf_op jit(solution)/shard_map/ppermute | solution.py:201
  107.8 113.1 %collective-permute-start.10 = (bf16[4,192,768]{2,1,0:T(8,128)(2,1)}, bf16[4,192,768]{2,1,0:T(8,128)(2,1)}, u32[]{:S(2)}, u32[]{:S(2)}) collective-permute-start(bf16[4,192,768]{2,1,0:T(8,128)(2,1)} %bitcast.377), channel_id=1, source_target_pairs={{0,1},{1,0},{2,3},{3,2},{4,5},{5,4},{6,7},{7,6},{8,9},{9,8},{10,11... | collective-permute-start | bytes 3538952 | tf_op jit(solution)/shard_map/ppermute | solution.py:179
  220.9 58.6 %collective-permute-start.17 = (bf16[4,192,768]{2,1,0:T(8,128)(2,1)S(1)}, bf16[4,192,768]{2,1,0:T(8,128)(2,1)}, u32[]{:S(2)}, u32[]{:S(2)}) collective-permute-start(bf16[4,192,768]{2,1,0:T(8,128)(2,1)S(1)} %bitcast.372), channel_id=1, source_target_pairs={{0,16},{16,0},{1,17},{17,1},{2,18},{18,2},{3,19},{19,3},{4,20},{20... | collective-permute-start | bytes 3538952 | tf_op jit(solution)/shard_map/ppermute | solution.py:201
  228.9 63.0 %collective-permute-start.19 = (bf16[4,192,768]{2,1,0:T(8,128)(2,1)S(1)}, bf16[4,192,768]{2,1,0:T(8,128)(2,1)}, u32[]{:S(2)}, u32[]{:S(2)}) collective-permute-start(bf16[4,192,768]{2,1,0:T(8,128)(2,1)S(1)} %bitcast.368), channel_id=1, source_target_pairs={{0,1},{1,0},{2,3},{3,2},{4,5},{5,4},{6,7},{7,6},{8,9},{9,8},{10,11... | collective-permute-start | bytes 3538952 | tf_op jit(solution)/shard_map/ppermute | solution.py:179
  232.8 71.9 %collective-permute-start.20 = (bf16[4,192,768]{2,1,0:T(8,128)(2,1)S(1)}, bf16[4,192,768]{2,1,0:T(8,128)(2,1)}, u32[]{:S(2)}, u32[]{:S(2)}) collective-permute-start(bf16[4,192,768]{2,1,0:T(8,128)(2,1)S(1)} %bitcast.369), channel_id=1, source_target_pairs={{0,16},{16,0},{1,17},{17,1},{2,18},{18,2},{3,19},{19,3},{4,20},{20... | collective-permute-start | bytes 3538952 | tf_op jit(solution)/shard_map/ppermute | solution.py:201
  254.2 52.7 %collective-permute-start.4 = (bf16[4,192,768]{2,1,0:T(8,128)(2,1)}, bf16[4,192,768]{2,1,0:T(8,128)(2,1)}, u32[]{:S(2)}, u32[]{:S(2)}) collective-permute-start(bf16[4,192,768]{2,1,0:T(8,128)(2,1)} %collective-permute-done.3), channel_id=1, source_target_pairs={{0,1},{1,0},{2,3},{3,2},{4,5},{5,4},{6,7},{7,6},{8,9},{9,8},{10,11... | collective-permute-start | bytes 3538952 | tf_op jit(solution)/shard_map/ppermute | solution.py:179
  685.8 125.7 %all-gather.36.cloned.1.call-start = ((), (), s32[]{:S(2)}) async-start(), calls=%async_computation.11 | async-start | bytes 3932160 | tf_op jit(solution)/shard_map/all_gather | solution.py:176
  729.9 197.6 %all-gather.40.cloned.1.call-start = ((), (), s32[]{:S(2)}) async-start(), calls=%async_computation.13 | async-start | bytes 7864320 | tf_op jit(solution)/shard_map/all_gather | solution.py:176
  730.7 284.4 %reduce-scatter.3.cloned.1.call-start = ((), (), s32[]{:S(2)}) async-start(), calls=%async_computation.2 | async-start | bytes 6021120 | tf_op jit(solution)/shard_map/reduce_scatter | solution.py:273
  752.5 352.9 %reduce-scatter.5.cloned.1.call-start = ((), (), s32[]{:S(2)}) async-start(), calls=%async_computation.3 | async-start | bytes 6021120 | tf_op jit(solution)/shard_map/reduce_scatter | solution.py:272
  753.2 470.3 %all-gather.34.cloned.1.call-start = ((), (), s32[]{:S(2)}) async-start(), calls=%async_computation.10 | async-start | bytes 7864320 | tf_op jit(solution)/shard_map/all_gather | solution.py:176
  753.3 59.2 %collective-permute-start.28 = (bf16[4,512,768]{2,1,0:T(8,128)(2,1)}, bf16[4,512,768]{2,1,0:T(8,128)(2,1)}, u32[]{:S(2)}, u32[]{:S(2)}) collective-permute-start(bf16[4,512,768]{2,1,0:T(8,128)(2,1)} %bitcast.358), channel_id=1, source_target_pairs={{0,1},{1,0},{2,3},{3,2},{4,5},{5,4},{6,7},{7,6},{8,9},{9,8},{10,11... | collective-permute-start | bytes 9437192 | tf_op jit(solution)/shard_map/ppermute | solution.py:179
  811.6 119.6 %collective-permute-start.27 = (bf16[4,512,768]{2,1,0:T(8,128)(2,1)}, bf16[4,512,768]{2,1,0:T(8,128)(2,1)}, u32[]{:S(2)}, u32[]{:S(2)}) collective-permute-start(bf16[4,512,768]{2,1,0:T(8,128)(2,1)} %bitcast.360), channel_id=1, source_target_pairs={{0,1},{1,0},{2,3},{3,2},{4,5},{5,4},{6,7},{7,6},{8,9},{9,8},{10,11... | collective-permute-start | bytes 9437192 | tf_op jit(solution)/shard_map/ppermute | solution.py:179
  940.2 299.9 %collective-permute-start.31 = (bf16[4,2,512,768]{3,2,1,0:T(8,128)(2,1)}, bf16[4,2,512,768]{3,2,1,0:T(8,128)(2,1)}, u32[]{:S(2)}, u32[]{:S(2)}) collective-permute-start(bf16[4,2,512,768]{3,2,1,0:T(8,128)(2,1)} %pad_maximum_fusion.1), channel_id=1, source_target_pairs={{2,1},{6,5},{10,9},{14,13},{18,17},{22,21},{26,25},{30,29}} | collective-permute-start | bytes 18874376 | tf_op jit(solution)/shard_map/ppermute | solution.py:276
  1107.9 124.3 %collective-permute-start.30 = (f32[392,768]{1,0:T(8,128)}, f32[392,768]{1,0:T(8,128)}, u32[]{:S(2)}, u32[]{:S(2)}) collective-permute-start(f32[392,768]{1,0:T(8,128)} %select_bitcast_fusion), channel_id=1, source_target_pairs={{0,1},{1,0},{2,3},{3,2},{4,5},{5,4},{6,7},{7,6},{8,9},{9,8},{10,11... | collective-permute-start | bytes 3612680 | tf_op jit(solution)/shard_map/ppermute | solution.py:179
  (127 other events, 1817.8 us)
Sparse Core Ops, SparseCore 0:
  12.3 31.7 all-gather.21
  46.2 29.8 all-gather.23
  78.3 29.5 all-gather.25
  109.8 29.4 all-gather.27
  141.3 29.4 all-gather.29
  172.8 29.4 all-gather.31
  686.0 61.8 all-gather.37
  749.5 62.0 all-gather.35
  813.2 114.2 all-gather.39
  930.2 84.8 reduce-scatter.2
  1018.0 87.3 reduce-scatter.4
  1107.4 116.0 all-gather.33

commit v3 on v2

--- a/solution.py
+++ b/solution.py
@@ -195,7 +195,11 @@
             pieces[0].append(by_core(mine, got))
             pieces[1].append(by_core(got, mine))
 
-        gathered = [gather_tp(piece) for piece in pieces[0] + pieces[1]]
+        groups = (pieces[0][0][None], jnp.stack(pieces[0][1:]), jnp.stack(pieces[1]))
+        gathered = []
+        for group in groups:
+            whole = gather_tp(group)
+            gathered += [whole[:, j] for j in range(group.shape[0])]
         from_x = []
         for own_x in gathered:
             from_x.append(lax.ppermute(own_x, 'dp', swap))
@@ -230,19 +234,25 @@
         def pair_pick(phase_a, phase_b):
             return jnp.where(first_pair, phase_a, phase_b)
 
+        def hop(value, source):
+            return lax.ppermute(value, 'py', [(source, 1 - source)])
+
         outs_a, saved_a = forward(my_sequence(x_in))
-        outs_b, saved_b = forward(lax.ppermute(outs_a[1], 'py', [(0, 1)]))
-
-        def own_stage(phase_a, phase_b):
-            layers = [pair_pick(phase_a[layer], phase_b[layer]) for layer in range(2)]
+        outs_b, saved_b = forward(hop(outs_a[1], 0))
+
+        def split_gather(outs, saved, source):
+            layers = [jnp.stack([outs[layer], saved[layer][4]]) for layer in range(2)]
             keep, other = by_core(*layers), core_swap(by_core(layers[1], layers[0]))
-            return jnp.stack([by_core(keep, other), by_core(other, keep)])
-
-        own_out = own_stage(outs_a, outs_b)
-        own_mid = own_stage([saved[4] for saved in saved_a], [saved[4] for saved in saved_b])
-        g_top, own_out, own_mid = lax.optimization_barrier((my_sequence(dy_out), own_out, own_mid))
-        stage_out = gather_tp(own_out)
-        mid_all = gather_tp(own_mid)
+            row0, row1 = by_core(keep, other), by_core(other, keep)
+            moved = hop(row1, source)
+            near = gather_tp(jnp.where(py_id == source, row0, moved))
+            return near, hop(near, 1 - source)
+
+        near_a, far_a = split_gather(outs_a, saved_a, 0)
+        near_b, far_b = split_gather(outs_b, saved_b, 1)
+        row_sets = pair_pick(near_a, near_b), pair_pick(far_a, far_b)
+        stage_out, mid_all = (jnp.stack([row_set[:, i] for row_set in row_sets], axis=1) for i in range(2))
+        g_top = my_sequence(dy_out)
 
         def weight_payload(keep_a, keep_b):
             d_qkv_a, d_qkv_b = keep_a[0], keep_b[0]
@@ -263,14 +273,15 @@
 
         dx1_b, keep1_b = layer_backward(g_top, saved_b[1], params[1], length)
         dx0_b, keep0_b = layer_backward(dx1_b, saved_b[0], params[0], length)
-        dx1_a, keep1_a = layer_backward(lax.ppermute(dx0_b, 'py', [(1, 0)]), saved_a[1], params[1], length)
+        dx1_a, keep1_a = layer_backward(hop(dx0_b, 1), saved_a[1], params[1], length)
         own_dx1, dx1_a, keep1_a = lax.optimization_barrier((pair_pick(dx1_a, dx1_b), dx1_a, keep1_a))
         dx1_all = both_rows(gather_tp(own_dx1))
         dx0_a, keep0_a = layer_backward(dx1_a, saved_a[0], params[0], length)
         own_dx0, payload1 = lax.optimization_barrier((pair_pick(dx0_a, dx0_b), weight_payload(keep1_a, keep1_b)))
         dx0_all = both_rows(gather_tp(own_dx0))
         reduced1 = lax.psum_scatter(payload1, 'tp', scatter_dimension=0, tiled=False)
-        reduced0 = lax.psum_scatter(weight_payload(keep0_a, keep0_b), 'tp', scatter_dimension=0, tiled=False)
+        payload0 = weight_payload(keep0_a, keep0_b)
+        reduced0 = lax.psum_scatter(payload0, 'tp', scatter_dimension=0, tiled=False)
 
         stage_dx = by_core(dx0_all, dx1_all)
         from_next = lax.ppermute(dx0_all, pp, [(2, 1)])

time: 1290 us -> 1240 us (0.961)
  waiting for transfers between devices: 664 us -> 610 us
  other arithmetic: 102 us -> 115 us
    all_gather x10 -> x7, waiting for transfers between devices: 427 us -> 266 us  [gather_tp(): return lax.all_gather(value, 'tp', axis=0)]
    ppermute x2 -> x6, waiting for transfers between devices: 35.8 us -> 104 us  [hop(): return lax.ppermute(value, 'py', [(source, 1 - source)])]
    ppermute x6, waiting for transfers between devices: 42.5 us -> 67.5 us  [compute(): from_x.append(lax.ppermute(own_x, 'dp', swap))]
  transfers between devices with their start and end apart: 44 -> 45, of which waited for: 20 -> 20; matrix products, arithmetic and copies ran while one was open for 16% -> 17% of each run, Pallas kernels for 1% -> 3%
where the time goes in v3:
time: 1240 us
  waiting for transfers between devices  610 us (49%)
  matrix products  209 us (17%)
  Pallas kernels  129 us (10%)
  other arithmetic  115 us (9%)
  local copies, waits for them, and re-layouts  105 us (8%)
  starting transfers between devices  41.2 us (3%)
  between operations  16.1 us (1%)
    all_gather x7, waiting for transfers between devices, gather_tp(): return lax.all_gather(value, 'tp', axis=0)  266 us
    dot_general x40, matrix products, dot(): return lax.dot_general(lhs, rhs, dims, preferred_element_type=F32)  209 us
    ppermute x6, waiting for transfers between devices, hop(): return lax.ppermute(value, 'py', [(source, 1 - source)])  104 us
    reduce_scatter x1, waiting for transfers between devices, compute(): lax.psum_scatter(payload1, 'tp', scatter_dimension=0, tiled=False)  90.3 us
    pallas_call x4, Pallas kernels, attn_bwd(): pl.pallas_call(attn_bwd_kernel, grid=(pairs,), out_shape=jax.ShapeDtypeSt...  76.5 us
    reduce_scatter x1, waiting for transfers between devices, compute(): lax.psum_scatter(payload0, 'tp', scatter_dimension=0, tiled=False)  70.9 us
    ppermute x6, waiting for transfers between devices, compute(): from_x.append(lax.ppermute(own_x, 'dp', swap))  67.5 us
    pallas_call x4, Pallas kernels, attn_fwd(): pl.pallas_call(attn_fwd_kernel, grid=(pairs,), out_shape=jax.ShapeDtypeSt...  52.4 us
  transfers between devices with their start and end apart: 45, of which 20 were waited for; matrix products, arithmetic and copies ran while one was open for 17% of the time, Pallas kernels for 3%

profile of v3, /device:TPU:1, one launch (start us, length us, event | category | flops | bytes accessed | tf_op | source)
XLA Modules:
  0.0 1236.8 jit_solution(9735342817598632374)
XLA Ops:
  17.8 26.2 %all-gather.16.cloned.1.call-done = bf16[768,768]{1,0:T(8,128)(2,1)} async-done(((bf16[192,768]{1,0:T(8,128)(2,1)}), bf16[768,768]{1,0:T(8,128)(2,1)}) %all-gather.16.cloned.1.call-update) | async-done | bytes 1179664 | tf_op jit(solution)/shard_map/all_gather | solution.py:176
  80.0 16.2 %all-gather.18.cloned.1.call-done = bf16[8,192,768]{2,1,0:T(8,128)(2,1)} async-done(((bf16[2,192,768]{2,1,0:T(8,128)(2,1)}), bf16[8,192,768]{2,1,0:T(8,128)(2,1)}) %all-gather.18.cloned.1.call-update) | async-done | bytes 2359312 | tf_op jit(solution)/shard_map/all_gather | solution.py:176
  114.7 13.1 %attn_fwd.4 = bf16[512,768]{1,0:T(8,128)(2,1)} custom-call(s32[1]{0:T(128)} %bitcast.1.len_ref, bf16[512,2304]{1,0:T(8,128)(2,1)} %fusion.37.q_ref.k_ref.v_ref, bf16[512,2304]{1,0:T(8,128)(2,1)} %fusion.37.q_ref.k_ref.v_ref, bf16[512,2304]{1,0:T(8,128)(2,1)} %fusion.37.q_ref.k_ref.v_ref), custom_call_target="tpu_custom_call" | custom-call | flops 3221225472 | bytes 3145728 | tf_op jit(solution)/shard_map/attn_fwd/pallas_call | solution.py:71
  130.9 22.1 %collective-permute-done.11 = bf16[4,192,768]{2,1,0:T(8,128)(2,1)} collective-permute-done((bf16[4,192,768]{2,1,0:T(8,128)(2,1)S(1)}, bf16[4,192,768]{2,1,0:T(8,128)(2,1)}, u32[]{:S(2)}, u32[]{:S(2)}) %collective-permute-start.11) | collective-permute-done | bytes 1179680 | tf_op jit(solution)/shard_map/ppermute | solution.py:205
  208.7 16.7 %collective-permute-done.17 = bf16[4,192,768]{2,1,0:T(8,128)(2,1)} collective-permute-done((bf16[4,192,768]{2,1,0:T(8,128)(2,1)}, bf16[4,192,768]{2,1,0:T(8,128)(2,1)}, u32[]{:S(2)}, u32[]{:S(2)}) %collective-permute-start.17) | collective-permute-done | bytes 1179680 | tf_op jit(solution)/shard_map/ppermute | solution.py:205
  226.6 24.0 %collective-permute-done.20 = bf16[4,192,768]{2,1,0:T(8,128)(2,1)} collective-permute-done((bf16[4,192,768]{2,1,0:T(8,128)(2,1)S(1)}, bf16[4,192,768]{2,1,0:T(8,128)(2,1)}, u32[]{:S(2)}, u32[]{:S(2)}) %collective-permute-start.20) | collective-permute-done | bytes 1179680 | tf_op jit(solution)/shard_map/ppermute | solution.py:205
  276.0 13.1 %attn_fwd.5 = bf16[512,768]{1,0:T(8,128)(2,1)} custom-call(s32[1]{0:T(128)} %bitcast.1.len_ref, bf16[512,2304]{1,0:T(8,128)(2,1)} %fusion.38.q_ref.k_ref.v_ref, bf16[512,2304]{1,0:T(8,128)(2,1)} %fusion.38.q_ref.k_ref.v_ref, bf16[512,2304]{1,0:T(8,128)(2,1)} %fusion.38.q_ref.k_ref.v_ref), custom_call_target="tpu_custom_call" | custom-call | flops 3221225472 | bytes 3145728 | tf_op jit(solution)/shard_map/attn_fwd/pallas_call | solution.py:71
  312.4 16.8 %collective-permute-done.24 = bf16[512,768]{1,0:T(8,128)(2,1)S(1)} collective-permute-done((bf16[512,768]{1,0:T(8,128)(2,1)S(1)}, bf16[512,768]{1,0:T(8,128)(2,1)S(1)}, u32[]{:S(2)}, u32[]{:S(2)}) %collective-permute-start.24) | collective-permute-done | bytes 786464 | tf_op jit(solution)/shard_map/ppermute | solution.py:238
  333.4 13.1 %attn_fwd.6 = bf16[512,768]{1,0:T(8,128)(2,1)} custom-call(s32[1]{0:T(128)} %bitcast.1.len_ref, bf16[512,2304]{1,0:T(8,128)(2,1)} %fusion.39.q_ref.k_ref.v_ref, bf16[512,2304]{1,0:T(8,128)(2,1)} %fusion.39.q_ref.k_ref.v_ref, bf16[512,2304]{1,0:T(8,128)(2,1)} %fusion.39.q_ref.k_ref.v_ref), custom_call_target="tpu_custom_call" | custom-call | flops 3221225472 | bytes 3145728 | tf_op jit(solution)/shard_map/attn_fwd/pallas_call | solution.py:71
  365.9 13.1 %attn_fwd.7 = bf16[512,768]{1,0:T(8,128)(2,1)} custom-call(s32[1]{0:T(128)} %bitcast.1.len_ref, bf16[512,2304]{1,0:T(8,128)(2,1)} %fusion.40.q_ref.k_ref.v_ref, bf16[512,2304]{1,0:T(8,128)(2,1)} %fusion.40.q_ref.k_ref.v_ref, bf16[512,2304]{1,0:T(8,128)(2,1)} %fusion.40.q_ref.k_ref.v_ref), custom_call_target="tpu_custom_call" | custom-call | flops 3221225472 | bytes 3145728 | tf_op jit(solution)/shard_map/attn_fwd/pallas_call | solution.py:71
  389.5 12.4 %fusion.191 = (f32[768]{0:T(1024)S(1)}, f32[512]{0:T(512)S(1)}, f32[512]{0:T(512)S(1)}, f32[768]{0:T(1024)S(1)}, bf16[512,768]{1,0:T(8,128)(2,1)}) fusion(bf16[512,768]{1,0:T(8,128)(2,1)} %copy-done.4, f32[512]{0:T(512)S(1)} %add_rsqrt_fusion.1, f32[512]{0:T(512)S(1)} %broadcast_multiply_fusion.17, f32[768]{0:T(1024)S(1)} %get-tuple-element.204, ...), kind=kOutput, calls=%fused_computation.299 | convolution fusion | flops 4857000960 | bytes 18117640 | tf_op jit(solution)/shard_map/dot_general | solution.py:20
  406.9 19.4 %attn_bwd.4 = bf16[512,2304]{1,0:T(8,128)(2,1)} custom-call(s32[1]{0:T(128)} %bitcast.1.len_ref, bf16[512,2304]{1,0:T(8,128)(2,1)} %fusion.40.q_ref.k_ref.v_ref, bf16[512,2304]{1,0:T(8,128)(2,1)} %fusion.40.q_ref.k_ref.v_ref, bf16[512,2304]{1,0:T(8,128)(2,1)} %fusion.40.q_ref.k_ref.v_ref, bf16[512,768]{1,0:T(8,128)(2,1)} %convolution_convert_fusion.8.dctx_ref), custom_call_target="tpu_custom_call" | custom-call | flops 8053063680 | bytes 5505024 | tf_op jit(solution)/shard_map/attn_bwd/pallas_call | solution.py:85
  433.0 12.1 fusion.193
  450.0 19.2 %attn_bwd.5 = bf16[512,2304]{1,0:T(8,128)(2,1)} custom-call(s32[1]{0:T(128)} %bitcast.1.len_ref, bf16[512,2304]{1,0:T(8,128)(2,1)} %fusion.39.q_ref.k_ref.v_ref, bf16[512,2304]{1,0:T(8,128)(2,1)} %fusion.39.q_ref.k_ref.v_ref, bf16[512,2304]{1,0:T(8,128)(2,1)} %fusion.39.q_ref.k_ref.v_ref, bf16[512,768]{1,0:T(8,128)(2,1)} %convolution_convert_fusion.7.dctx_ref), custom_call_target="tpu_custom_call" | custom-call | flops 8053063680 | bytes 5505024 | tf_op jit(solution)/shard_map/attn_bwd/pallas_call | solution.py:85
  479.4 17.1 %collective-permute-done.29 = bf16[512,768]{1,0:T(8,128)(2,1)S(1)} collective-permute-done((bf16[512,768]{1,0:T(8,128)(2,1)}, bf16[512,768]{1,0:T(8,128)(2,1)S(1)}, u32[]{:S(2)}, u32[]{:S(2)}) %collective-permute-start.29) | collective-permute-done | bytes 786464 | tf_op jit(solution)/shard_map/ppermute | solution.py:238
  512.9 19.0 %attn_bwd.6 = bf16[512,2304]{1,0:T(8,128)(2,1)} custom-call(s32[1]{0:T(128)} %bitcast.1.len_ref, bf16[512,2304]{1,0:T(8,128)(2,1)} %fusion.38.q_ref.k_ref.v_ref, bf16[512,2304]{1,0:T(8,128)(2,1)} %fusion.38.q_ref.k_ref.v_ref, bf16[512,2304]{1,0:T(8,128)(2,1)} %fusion.38.q_ref.k_ref.v_ref, bf16[512,768]{1,0:T(8,128)(2,1)} %convolution_convert_fusion.6.dctx_ref), custom_call_target="tpu_custom_call" | custom-call | flops 8053063680 | bytes 5505024 | tf_op jit(solution)/shard_map/attn_bwd/pallas_call | solution.py:85
  550.6 12.1 fusion.197
  568.8 19.0 %attn_bwd.7 = bf16[512,2304]{1,0:T(8,128)(2,1)} custom-call(s32[1]{0:T(128)} %bitcast.1.len_ref, bf16[512,2304]{1,0:T(8,128)(2,1)} %fusion.37.q_ref.k_ref.v_ref, bf16[512,2304]{1,0:T(8,128)(2,1)} %fusion.37.q_ref.k_ref.v_ref, bf16[512,2304]{1,0:T(8,128)(2,1)} %fusion.37.q_ref.k_ref.v_ref, bf16[512,768]{1,0:T(8,128)(2,1)} %convolution_convert_fusion.5.dctx_ref), custom_call_target="tpu_custom_call" | custom-call | flops 8053063680 | bytes 5505024 | tf_op jit(solution)/shard_map/attn_bwd/pallas_call | solution.py:85
  614.0 33.6 %collective-permute-done.23 = bf16[2,512,768]{2,1,0:T(8,128)(2,1)S(1)} collective-permute-done((bf16[2,512,768]{2,1,0:T(8,128)(2,1)S(1)}, bf16[2,512,768]{2,1,0:T(8,128)(2,1)S(1)}, u32[]{:S(2)}, u32[]{:S(2)}) %collective-permute-start.23) | collective-permute-done | bytes 1572896 | tf_op jit(solution)/shard_map/ppermute | solution.py:238
  663.3 36.8 %collective-permute-done.26 = bf16[2,512,768]{2,1,0:T(8,128)(2,1)} collective-permute-done((bf16[2,512,768]{2,1,0:T(8,128)(2,1)}, bf16[2,512,768]{2,1,0:T(8,128)(2,1)}, u32[]{:S(2)}, u32[]{:S(2)}) %collective-permute-start.26) | collective-permute-done | bytes 1572896 | tf_op jit(solution)/shard_map/ppermute | solution.py:238
  742.6 105.1 %all-gather.22.cloned.1.call-done = bf16[8,512,768]{2,1,0:T(8,128)(2,1)} async-done(((bf16[2,512,768]{2,1,0:T(8,128)(2,1)}), bf16[8,512,768]{2,1,0:T(8,128)(2,1)}) %all-gather.22.cloned.1.call-update) | async-done | bytes 6291472 | tf_op jit(solution)/shard_map/all_gather | solution.py:176
  849.0 114.4 %all-gather.24.cloned.1.call-done = bf16[8,512,768]{2,1,0:T(8,128)(2,1)} async-done(((bf16[2,512,768]{2,1,0:T(8,128)(2,1)}), bf16[8,512,768]{2,1,0:T(8,128)(2,1)}) %all-gather.24.cloned.1.call-update) | async-done | bytes 6291472 | tf_op jit(solution)/shard_map/all_gather | solution.py:176
  979.6 70.9 %reduce-scatter.3.cloned.1.call-done = f32[1,392,768]{2,1,0:T(8,128)} async-done(((f32[4,392,768]{2,1,0:T(8,128)}), f32[1,392,768]{2,1,0:T(8,128)}) %reduce-scatter.3.cloned.1.call-update) | async-done | bytes 1204240 | tf_op jit(solution)/shard_map/reduce_scatter | solution.py:284
  1050.6 90.3 %reduce-scatter.5.cloned.1.call-done = f32[1,392,768]{2,1,0:T(8,128)} async-done(((f32[4,392,768]{2,1,0:T(8,128)}), f32[1,392,768]{2,1,0:T(8,128)}) %reduce-scatter.5.cloned.1.call-update) | async-done | bytes 1204240 | tf_op jit(solution)/shard_map/reduce_scatter | solution.py:282
  (525 shorter events, 464.8 us)
Async XLA Ops:
  7.2 36.8 %all-gather.16.cloned.1.call-start = ((), (), s32[]{:S(2)}) async-start(), calls=%async_computation.4 | async-start | bytes 1474560 | tf_op jit(solution)/shard_map/all_gather | solution.py:176
  12.1 84.2 %all-gather.18.cloned.1.call-start = ((), (), s32[]{:S(2)}) async-start(), calls=%async_computation.5 | async-start | bytes 2949120 | tf_op jit(solution)/shard_map/all_gather | solution.py:176
  17.7 150.3 %all-gather.20.cloned.1.call-start = ((), (), s32[]{:S(2)}) async-start(), calls=%async_computation.6 | async-start | bytes 4423680 | tf_op jit(solution)/shard_map/all_gather | solution.py:176
  64.6 662.2 %all-gather.26.cloned.1.call-start = ((), (), s32[]{:S(2)}) async-start(), calls=%async_computation.9 | async-start | bytes 3932160 | tf_op jit(solution)/shard_map/all_gather | solution.py:176
  99.0 31.8 %collective-permute-start.7 = (bf16[4,192,768]{2,1,0:T(8,128)(2,1)}, bf16[4,192,768]{2,1,0:T(8,128)(2,1)}, u32[]{:S(2)}, u32[]{:S(2)}) collective-permute-start(bf16[4,192,768]{2,1,0:T(8,128)(2,1)} %get-tuple-element.81), channel_id=1, source_target_pairs={{0,1},{1,0},{2,3},{3,2},{4,5},{5,4},{6,7},{7,6},{8,9},{9,8},{10,11... | collective-permute-start | bytes 3538952 | tf_op jit(solution)/shard_map/ppermute | solution.py:179
  101.2 51.7 %collective-permute-start.11 = (bf16[4,192,768]{2,1,0:T(8,128)(2,1)S(1)}, bf16[4,192,768]{2,1,0:T(8,128)(2,1)}, u32[]{:S(2)}, u32[]{:S(2)}) collective-permute-start(bf16[4,192,768]{2,1,0:T(8,128)(2,1)S(1)} %get-tuple-element.89), channel_id=1, source_target_pairs={{0,16},{16,0},{1,17},{17,1},{2,18},{18,2},{3,19},{19,3},{4,20},{20... | collective-permute-start | bytes 3538952 | tf_op jit(solution)/shard_map/ppermute | solution.py:205
  101.3 51.7 %collective-permute-start.10 = (bf16[4,192,768]{2,1,0:T(8,128)(2,1)S(1)}, bf16[4,192,768]{2,1,0:T(8,128)(2,1)}, u32[]{:S(2)}, u32[]{:S(2)}) collective-permute-start(bf16[4,192,768]{2,1,0:T(8,128)(2,1)S(1)} %get-tuple-element.89), channel_id=1, source_target_pairs={{0,1},{1,0},{2,3},{3,2},{4,5},{5,4},{6,7},{7,6},{8,9},{9,8},{10,11... | collective-permute-start | bytes 3538952 | tf_op jit(solution)/shard_map/ppermute | solution.py:179
  173.9 51.4 %collective-permute-start.17 = (bf16[4,192,768]{2,1,0:T(8,128)(2,1)}, bf16[4,192,768]{2,1,0:T(8,128)(2,1)}, u32[]{:S(2)}, u32[]{:S(2)}) collective-permute-start(bf16[4,192,768]{2,1,0:T(8,128)(2,1)} %get-tuple-element.105), channel_id=1, source_target_pairs={{0,16},{16,0},{1,17},{17,1},{2,18},{18,2},{3,19},{19,3},{4,20},{20... | collective-permute-start | bytes 3538952 | tf_op jit(solution)/shard_map/ppermute | solution.py:205
  173.9 79.9 %collective-permute-start.19 = (bf16[4,192,768]{2,1,0:T(8,128)(2,1)S(1)}, bf16[4,192,768]{2,1,0:T(8,128)(2,1)}, u32[]{:S(2)}, u32[]{:S(2)}) collective-permute-start(bf16[4,192,768]{2,1,0:T(8,128)(2,1)S(1)} %get-tuple-element.113), channel_id=1, source_target_pairs={{0,1},{1,0},{2,3},{3,2},{4,5},{5,4},{6,7},{7,6},{8,9},{9,8},{10,11... | collective-permute-start | bytes 3538952 | tf_op jit(solution)/shard_map/ppermute | solution.py:179
  192.8 57.8 %collective-permute-start.20 = (bf16[4,192,768]{2,1,0:T(8,128)(2,1)S(1)}, bf16[4,192,768]{2,1,0:T(8,128)(2,1)}, u32[]{:S(2)}, u32[]{:S(2)}) collective-permute-start(bf16[4,192,768]{2,1,0:T(8,128)(2,1)S(1)} %get-tuple-element.113), channel_id=1, source_target_pairs={{0,16},{16,0},{1,17},{17,1},{2,18},{18,2},{3,19},{19,3},{4,20},{20... | collective-permute-start | bytes 3538952 | tf_op jit(solution)/shard_map/ppermute | solution.py:205
  201.7 60.6 %collective-permute-start.15 = (bf16[4,192,768]{2,1,0:T(8,128)(2,1)}, bf16[4,192,768]{2,1,0:T(8,128)(2,1)}, u32[]{:S(2)}, u32[]{:S(2)}) collective-permute-start(bf16[4,192,768]{2,1,0:T(8,128)(2,1)} %collective-permute-done.14), channel_id=1, source_target_pairs={{0,1},{1,0},{2,3},{3,2},{4,5},{5,4},{6,7},{7,6},{8,9},{9,8},{10,11... | collective-permute-start | bytes 3538952 | tf_op jit(solution)/shard_map/ppermute | solution.py:179
  225.3 44.8 %collective-permute-start.18 = (bf16[4,192,768]{2,1,0:T(8,128)(2,1)}, bf16[4,192,768]{2,1,0:T(8,128)(2,1)}, u32[]{:S(2)}, u32[]{:S(2)}) collective-permute-start(bf16[4,192,768]{2,1,0:T(8,128)(2,1)} %collective-permute-done.17), channel_id=1, source_target_pairs={{0,1},{1,0},{2,3},{3,2},{4,5},{5,4},{6,7},{7,6},{8,9},{9,8},{10,11... | collective-permute-start | bytes 3538952 | tf_op jit(solution)/shard_map/ppermute | solution.py:179
  549.0 50.4 %collective-permute-start.30 = (bf16[4,512,768]{2,1,0:T(8,128)(2,1)}, bf16[4,512,768]{2,1,0:T(8,128)(2,1)}, u32[]{:S(2)}, u32[]{:S(2)}) collective-permute-start(bf16[4,512,768]{2,1,0:T(8,128)(2,1)} %pad_maximum_fusion.2), channel_id=1, source_target_pairs={{0,1},{1,0},{2,3},{3,2},{4,5},{5,4},{6,7},{7,6},{8,9},{9,8},{10,11... | collective-permute-start | bytes 9437192 | tf_op jit(solution)/shard_map/ppermute | solution.py:179
  606.7 124.6 %all-gather.28.cloned.1.call-start = ((), (), s32[]{:S(2)}) async-start(), calls=%async_computation.10 | async-start | bytes 3932160 | tf_op jit(solution)/shard_map/all_gather | solution.py:176
  607.3 240.4 %all-gather.22.cloned.1.call-start = ((), (), s32[]{:S(2)}) async-start(), calls=%async_computation.7 | async-start | bytes 7864320 | tf_op jit(solution)/shard_map/all_gather | solution.py:176
  612.7 35.0 %collective-permute-start.23 = (bf16[2,512,768]{2,1,0:T(8,128)(2,1)S(1)}, bf16[2,512,768]{2,1,0:T(8,128)(2,1)S(1)}, u32[]{:S(2)}, u32[]{:S(2)}) collective-permute-start(bf16[2,512,768]{2,1,0:T(8,128)(2,1)S(1)} %broadcast_select_fusion.9), channel_id=1, source_target_pairs={{0,2},{1,3},{4,6},{5,7},{8,10},{9,11},{12,14},{13,15},{16,18},{17,... | collective-permute-start | bytes 4718600 | tf_op jit(solution)/shard_map/ppermute | solution.py:238
  649.1 314.2 %all-gather.24.cloned.1.call-start = ((), (), s32[]{:S(2)}) async-start(), calls=%async_computation.8 | async-start | bytes 7864320 | tf_op jit(solution)/shard_map/all_gather | solution.py:176
  662.0 38.1 %collective-permute-start.26 = (bf16[2,512,768]{2,1,0:T(8,128)(2,1)}, bf16[2,512,768]{2,1,0:T(8,128)(2,1)}, u32[]{:S(2)}, u32[]{:S(2)}) collective-permute-start(bf16[2,512,768]{2,1,0:T(8,128)(2,1)} %broadcast_select_fusion.6), channel_id=1, source_target_pairs={{2,0},{3,1},{6,4},{7,5},{10,8},{11,9},{14,12},{15,13},{18,16},{19,... | collective-permute-start | bytes 4718600 | tf_op jit(solution)/shard_map/ppermute | solution.py:238
  703.5 347.1 %reduce-scatter.3.cloned.1.call-start = ((), (), s32[]{:S(2)}) async-start(), calls=%async_computation.2 | async-start | bytes 6021120 | tf_op jit(solution)/shard_map/reduce_scatter | solution.py:284
  726.0 414.9 %reduce-scatter.5.cloned.1.call-start = ((), (), s32[]{:S(2)}) async-start(), calls=%async_computation.3 | async-start | bytes 6021120 | tf_op jit(solution)/shard_map/reduce_scatter | solution.py:282
  731.4 237.8 %collective-permute-start.32 = (bf16[4,512,768]{2,1,0:T(8,128)(2,1)}, bf16[4,512,768]{2,1,0:T(8,128)(2,1)}, u32[]{:S(2)}, u32[]{:S(2)}) collective-permute-start(bf16[4,512,768]{2,1,0:T(8,128)(2,1)} %bitcast.417), channel_id=1, source_target_pairs={{0,1},{1,0},{2,3},{3,2},{4,5},{5,4},{6,7},{7,6},{8,9},{9,8},{10,11... | collective-permute-start | bytes 9437192 | tf_op jit(solution)/shard_map/ppermute | solution.py:179
  741.3 419.6 %collective-permute-start.35 = (bf16[4,2,512,768]{3,2,0,1:T(8,128)(2,1)}, bf16[4,2,512,768]{3,2,0,1:T(8,128)(2,1)}, u32[]{:S(2)}, u32[]{:S(2)}) collective-permute-start(bf16[4,2,512,768]{3,2,0,1:T(8,128)(2,1)} %pad_maximum_fusion.1), channel_id=1, source_target_pairs={{2,1},{6,5},{10,9},{14,13},{18,17},{22,21},{26,25},{30,29}} | collective-permute-start | bytes 18874376 | tf_op jit(solution)/shard_map/ppermute | solution.py:287
  847.7 323.3 %collective-permute-start.27 = (bf16[4,2,512,768]{3,2,1,0:T(8,128)(2,1)}, bf16[4,2,512,768]{3,2,1,0:T(8,128)(2,1)}, u32[]{:S(2)}, u32[]{:S(2)}) collective-permute-start(bf16[4,2,512,768]{3,2,1,0:T(8,128)(2,1)} %bitcast.387), channel_id=1, source_target_pairs={{2,0},{3,1},{6,4},{7,5},{10,8},{11,9},{14,12},{15,13},{18,16},{19,... | collective-permute-start | bytes 18874376 | tf_op jit(solution)/shard_map/ppermute | solution.py:238
  963.4 207.6 %collective-permute-start.28 = (bf16[4,2,512,768]{3,2,1,0:T(8,128)(2,1)}, bf16[4,2,512,768]{3,2,1,0:T(8,128)(2,1)}, u32[]{:S(2)}, u32[]{:S(2)}) collective-permute-start(bf16[4,2,512,768]{3,2,1,0:T(8,128)(2,1)} %bitcast.389), channel_id=1, source_target_pairs={{0,2},{1,3},{4,6},{5,7},{8,10},{9,11},{12,14},{13,15},{16,18},{17,... | collective-permute-start | bytes 18874376 | tf_op jit(solution)/shard_map/ppermute | solution.py:238
  (115 other events, 2747.5 us)
Sparse Core Ops, SparseCore 0:
  12.2 31.7 all-gather.15
  46.1 50.0 all-gather.17
  98.4 68.9 all-gather.19
  606.9 60.9 all-gather.25
  669.2 62.0 all-gather.27
  733.4 114.2 all-gather.21
  849.8 113.5 all-gather.23
  965.7 84.8 reduce-scatter.2
  1053.5 87.3 reduce-scatter.4

commit v4 on v3

--- a/solution.py
+++ b/solution.py
@@ -8,6 +8,7 @@
 
 LN_EPS = 1e-5
 MASK_VALUE = -1e9
+SCALE = 0.125
 ROW_MAJOR = Layout((0, 1))
 F32 = jnp.float32
 BF16 = jnp.bfloat16
@@ -20,42 +21,43 @@
     return lax.dot_general(lhs, rhs, dims, preferred_element_type=F32)
 
 
+def key_major_probs(q_scaled, k, key_ok):
+    scores = jnp.where(key_ok, dot(k, q_scaled, NT), MASK_VALUE)
+    expd = jnp.exp(scores - jnp.max(scores, axis=0, keepdims=True))
+    return expd * (1.0 / jnp.sum(expd, axis=0, keepdims=True))
+
+
 def attn_fwd_kernel(len_ref, q_ref, k_ref, v_ref, ctx_ref):
     rows = q_ref.shape[0]
-    key_ok = lax.broadcasted_iota(jnp.int32, (rows, rows), 1) < len_ref[0]
+    key_ok = lax.broadcasted_iota(jnp.int32, (rows, rows), 0) < len_ref[0]
     parts = []
     for half in range(2):
         cols = slice(half * 64, half * 64 + 64)
-        scores = dot(q_ref[:, cols], k_ref[:, cols], NT) * 0.125
-        scores = jnp.where(key_ok, scores, MASK_VALUE)
-        expd = jnp.exp(scores - jnp.max(scores, axis=-1, keepdims=True))
-        prob = (expd * (1.0 / jnp.sum(expd, axis=-1, keepdims=True))).astype(BF16)
-        parts.append(dot(prob, v_ref[:, cols], NN).astype(BF16))
-    ctx_ref[...] = jnp.concatenate(parts, axis=1)
+        prob = key_major_probs(q_ref[:, cols] * SCALE, k_ref[:, cols], key_ok)
+        parts.append(dot(v_ref[:, cols], prob.astype(BF16), TN))
+    ctx_ref[...] = jnp.concatenate(parts, axis=0).T.astype(BF16)
 
 
 def attn_bwd_kernel(len_ref, q_ref, k_ref, v_ref, dctx_ref, dqkv_ref):
     rows = q_ref.shape[0]
     width = dqkv_ref.shape[1] // 3
     key_ok = lax.broadcasted_iota(jnp.int32, (rows, rows), 0) < len_ref[0]
-    pieces = ([], [], [])
+    d_q, d_k, d_v = [], [], []
     for half in range(2):
         cols = slice(half * 64, half * 64 + 64)
-        q, k, v, dctx = q_ref[:, cols], k_ref[:, cols], v_ref[:, cols], dctx_ref[:, cols]
-        scores = dot(k, q, NT) * 0.125
-        scores = jnp.where(key_ok, scores, MASK_VALUE)
-        expd = jnp.exp(scores - jnp.max(scores, axis=0, keepdims=True))
-        prob = expd * (1.0 / jnp.sum(expd, axis=0, keepdims=True))
+        q, k, v, dctx = q_ref[:, cols] * SCALE, k_ref[:, cols], v_ref[:, cols], dctx_ref[:, cols]
+        prob = key_major_probs(q, k, key_ok)
         d_prob = dot(v, dctx, NT)
         delta = jnp.sum(d_prob * prob, axis=0, keepdims=True)
-        d_scores = (prob * (d_prob - delta) * 0.125).astype(BF16)
-        pieces[0].append(dot(d_scores, k, TN).astype(BF16))
-        pieces[1].append(dot(d_scores, q, NN).astype(BF16))
-        pieces[2].append(dot(prob.astype(BF16), dctx, NN).astype(BF16))
+        d_scores = (prob * (d_prob - delta)).astype(BF16)
+        d_q.append(dot(k * SCALE, d_scores, TN))
+        d_k.append(dot(d_scores, q, NN).astype(BF16))
+        d_v.append(dot(prob.astype(BF16), dctx, NN).astype(BF16))
     pair = pl.program_id(0)
+    whole = (jnp.concatenate(d_q, axis=0).T.astype(BF16), jnp.concatenate(d_k, axis=1), jnp.concatenate(d_v, axis=1))
     for part in range(3):
         start = pl.multiple_of(part * width + pair * 128, 128)
-        dqkv_ref[:, pl.ds(start, 128)] = jnp.concatenate(pieces[part], axis=1)
+        dqkv_ref[:, pl.ds(start, 128)] = whole[part]
 
 
 def col_spec(rows, offset):
@@ -240,18 +242,18 @@
         outs_a, saved_a = forward(my_sequence(x_in))
         outs_b, saved_b = forward(hop(outs_a[1], 0))
 
-        def split_gather(outs, saved, source):
-            layers = [jnp.stack([outs[layer], saved[layer][4]]) for layer in range(2)]
-            keep, other = by_core(*layers), core_swap(by_core(layers[1], layers[0]))
-            row0, row1 = by_core(keep, other), by_core(other, keep)
-            moved = hop(row1, source)
-            near = gather_tp(jnp.where(py_id == source, row0, moved))
+        def split_gather(out, mid, source):
+            moved, out, pair_id = lax.optimization_barrier((hop(mid, source), out, py_id))
+            near = gather_tp(jnp.where(pair_id == source, out, moved))
             return near, hop(near, 1 - source)
 
-        near_a, far_a = split_gather(outs_a, saved_a, 0)
-        near_b, far_b = split_gather(outs_b, saved_b, 1)
-        row_sets = pair_pick(near_a, near_b), pair_pick(far_a, far_b)
-        stage_out, mid_all = (jnp.stack([row_set[:, i] for row_set in row_sets], axis=1) for i in range(2))
+        def own_rows(layer0, layer1):
+            keep, other = by_core(layer0, layer1), core_swap(by_core(layer1, layer0))
+            return jnp.stack([by_core(keep, other), by_core(other, keep)], axis=1)
+
+        moves_a = [split_gather(outs_a[layer], saved_a[layer][4], 0) for layer in range(2)]
+        moves_b = [split_gather(outs_b[layer], saved_b[layer][4], 1) for layer in range(2)]
+        stage_out, mid_all = (own_rows(*(pair_pick(moves_a[layer][i], moves_b[layer][i]) for layer in range(2))) for i in range(2))
         g_top = my_sequence(dy_out)
 
         def weight_payload(keep_a, keep_b):
@@ -279,9 +281,9 @@
         dx0_a, keep0_a = layer_backward(dx1_a, saved_a[0], params[0], length)
         own_dx0, payload1 = lax.optimization_barrier((pair_pick(dx0_a, dx0_b), weight_payload(keep1_a, keep1_b)))
         dx0_all = both_rows(gather_tp(own_dx0))
-        reduced1 = lax.psum_scatter(payload1, 'tp', scatter_dimension=0, tiled=False)
-        payload0 = weight_payload(keep0_a, keep0_b)
-        reduced0 = lax.psum_scatter(payload0, 'tp', scatter_dimension=0, tiled=False)
+        payload = jnp.concatenate([weight_payload(keep0_a, keep0_b), payload1], axis=1)
+        both_reduced = lax.psum_scatter(payload, 'tp', scatter_dimension=0, tiled=False)
+        reduced0, reduced1 = jnp.split(both_reduced, 2)
 
         stage_dx = by_core(dx0_all, dx1_all)
         from_next = lax.ppermute(dx0_all, pp, [(2, 1)])

time: 1240 us -> 968 us (0.78)
  waiting for transfers between devices: 610 us -> 262 us
  local copies, waits for them, and re-layouts: 105 us -> 130 us
  matrix products: 209 us -> 231 us
  starting transfers between devices: 41.2 us -> 62.4 us
  other arithmetic: 115 us -> 129 us
    all_gather x7 -> x9, waiting for transfers between devices: 266 us -> 56.4 us  [gather_tp(): return lax.all_gather(value, 'tp', axis=0)]
    reduce_scatter x2 -> x1, waiting for transfers between devices: 161 us -> 27.9 us  [compute(): lax.psum_scatter(payload, 'tp', scatter_dimension=0, tiled=False)]
    concatenate x0 -> x1, local copies, waits for them, and re-layouts: none -> 25 us  [compute(): jnp.concatenate([weight_payload(keep0_a, keep0_b), payload1], axis=1)]
    dot_general x40, matrix products: 209 us -> 231 us  [dot(): return lax.dot_general(lhs, rhs, dims, preferred_element_type=F32)]
    ppermute x1, waiting for transfers between devices: 0.01 us -> 17.9 us  [compute(): from_next = lax.ppermute(dx0_all, pp, [(2, 1)])]
    ppermute x6 -> x10, starting transfers between devices: 14.1 us -> 31.8 us  [hop(): return lax.ppermute(value, 'py', [(source, 1 - source)])]
    convert_element_type x0 -> x2, local copies, waits for them, and re-layouts: none -> 13.2 us  [the longest x1 10.2 us: normalise(): v = v_bf.astype(F32)]
    select_n x8 -> x6, other arithmetic: 6.63 us -> 19.8 us  [by_core(): return jnp.where(first_core, on_first, on_second)]
  transfers between devices with their start and end apart: 45 -> 50, of which waited for: 20 -> 19; matrix products, arithmetic and copies ran while one was open for 17% -> 49% of each run, Pallas kernels for 3% -> 12%
where the time goes in v4:
time: 968 us; the launch traced here: 959 us
  waiting for transfers between devices  262 us (27%)
  matrix products  231 us (24%)
  local copies, waits for them, and re-layouts  130 us (13%)
  other arithmetic  129 us (13%)
  Pallas kernels  118 us (12%)
  starting transfers between devices  62.4 us (6%)
  between operations  16.2 us (2%)
  blocking collectives  10.4 us (1%)
    dot_general x40, matrix products, dot(): return lax.dot_general(lhs, rhs, dims, preferred_element_type=F32)  231 us
    ppermute x10, waiting for transfers between devices, hop(): return lax.ppermute(value, 'py', [(source, 1 - source)])  94.8 us
    pallas_call x4, Pallas kernels, attn_bwd(): pl.pallas_call(attn_bwd_kernel, grid=(pairs,), out_shape=jax.ShapeDtypeSt...  74.4 us
    ppermute x6, waiting for transfers between devices, compute(): from_x.append(lax.ppermute(own_x, 'dp', swap))  62.4 us
    all_gather x9, waiting for transfers between devices, gather_tp(): return lax.all_gather(value, 'tp', axis=0)  56.4 us
    pallas_call x4, Pallas kernels, attn_fwd(): pl.pallas_call(attn_fwd_kernel, grid=(pairs,), out_shape=jax.ShapeDtypeSt...  43.3 us
    dynamic_update_slice x24, local copies, waits for them, and re-layouts, assemble(): full = lax.dynamic_update_index_in_dim(full, row, slot, 0)  42.1 us
    ppermute x10, starting transfers between devices, hop(): return lax.ppermute(value, 'py', [(source, 1 - source)])  31.8 us
  transfers between devices with their start and end apart: 50, of which 19 were waited for; matrix products, arithmetic and copies ran while one was open for 49% of the time, Pallas kernels for 12%

profile of v4, /device:TPU:1, one launch (start us, length us, event | category | flops | bytes accessed | tf_op | source)
XLA Modules:
  0.0 959.4 jit_solution(1444957162699156937)
XLA Ops:
  17.8 26.1 %all-gather.20.cloned.1.call-done = bf16[768,768]{1,0:T(8,128)(2,1)} async-done(((bf16[192,768]{1,0:T(8,128)(2,1)}), bf16[768,768]{1,0:T(8,128)(2,1)}) %all-gather.20.cloned.1.call-update) | async-done | bytes 1179664 | tf_op jit(solution)/shard_map/all_gather | solution.py:178
  82.3 13.9 %all-gather.22.cloned.1.call-done = bf16[8,192,768]{2,1,0:T(8,128)(2,1)} async-done(((bf16[2,192,768]{2,1,0:T(8,128)(2,1)}), bf16[8,192,768]{2,1,0:T(8,128)(2,1)}) %all-gather.22.cloned.1.call-update) | async-done | bytes 2359312 | tf_op jit(solution)/shard_map/all_gather | solution.py:178
  113.0 11.0 %attn_fwd.4 = bf16[512,768]{1,0:T(8,128)(2,1)} custom-call(s32[1]{0:T(128)} %bitcast.1.len_ref, bf16[512,2304]{1,0:T(8,128)(2,1)} %fusion.37.q_ref.k_ref.v_ref, bf16[512,2304]{1,0:T(8,128)(2,1)} %fusion.37.q_ref.k_ref.v_ref, bf16[512,2304]{1,0:T(8,128)(2,1)} %fusion.37.q_ref.k_ref.v_ref), custom_call_target="tpu_custom_call" | custom-call | flops 3221225472 | bytes 3145728 | tf_op jit(solution)/shard_map/attn_fwd/pallas_call | solution.py:73
  128.5 23.2 %collective-permute-done.12 = bf16[4,192,768]{2,1,0:T(8,128)(2,1)} collective-permute-done((bf16[4,192,768]{2,1,0:T(8,128)(2,1)S(1)}, bf16[4,192,768]{2,1,0:T(8,128)(2,1)}, u32[]{:S(2)}, u32[]{:S(2)}) %collective-permute-start.12) | collective-permute-done | bytes 1179680 | tf_op jit(solution)/shard_map/ppermute | solution.py:207
  213.1 11.5 %collective-permute-done.18 = bf16[4,192,768]{2,1,0:T(8,128)(2,1)} collective-permute-done((bf16[4,192,768]{2,1,0:T(8,128)(2,1)S(1)}, bf16[4,192,768]{2,1,0:T(8,128)(2,1)}, u32[]{:S(2)}, u32[]{:S(2)}) %collective-permute-start.18) | collective-permute-done | bytes 1179680 | tf_op jit(solution)/shard_map/ppermute | solution.py:207
  225.9 24.0 %collective-permute-done.21 = bf16[4,192,768]{2,1,0:T(8,128)(2,1)} collective-permute-done((bf16[4,192,768]{2,1,0:T(8,128)(2,1)S(1)}, bf16[4,192,768]{2,1,0:T(8,128)(2,1)}, u32[]{:S(2)}, u32[]{:S(2)}) %collective-permute-start.21) | collective-permute-done | bytes 1179680 | tf_op jit(solution)/shard_map/ppermute | solution.py:207
  276.4 10.8 %attn_fwd.5 = bf16[512,768]{1,0:T(8,128)(2,1)} custom-call(s32[1]{0:T(128)} %bitcast.1.len_ref, bf16[512,2304]{1,0:T(8,128)(2,1)} %fusion.38.q_ref.k_ref.v_ref, bf16[512,2304]{1,0:T(8,128)(2,1)} %fusion.38.q_ref.k_ref.v_ref, bf16[512,2304]{1,0:T(8,128)(2,1)} %fusion.38.q_ref.k_ref.v_ref), custom_call_target="tpu_custom_call" | custom-call | flops 3221225472 | bytes 3145728 | tf_op jit(solution)/shard_map/attn_fwd/pallas_call | solution.py:73
  314.4 12.1 %collective-permute-done.23 = bf16[512,768]{1,0:T(8,128)(2,1)S(1)} collective-permute-done((bf16[512,768]{1,0:T(8,128)(2,1)S(1)}, bf16[512,768]{1,0:T(8,128)(2,1)S(1)}, u32[]{:S(2)}, u32[]{:S(2)}) %collective-permute-start.23) | collective-permute-done | bytes 786464 | tf_op jit(solution)/shard_map/ppermute | solution.py:240
  332.7 10.8 %attn_fwd.6 = bf16[512,768]{1,0:T(8,128)(2,1)} custom-call(s32[1]{0:T(128)} %bitcast.1.len_ref, bf16[512,2304]{1,0:T(8,128)(2,1)} %fusion.39.q_ref.k_ref.v_ref, bf16[512,2304]{1,0:T(8,128)(2,1)} %fusion.39.q_ref.k_ref.v_ref, bf16[512,2304]{1,0:T(8,128)(2,1)} %fusion.39.q_ref.k_ref.v_ref), custom_call_target="tpu_custom_call" | custom-call | flops 3221225472 | bytes 3145728 | tf_op jit(solution)/shard_map/attn_fwd/pallas_call | solution.py:73
  366.5 10.8 %attn_fwd.7 = bf16[512,768]{1,0:T(8,128)(2,1)} custom-call(s32[1]{0:T(128)} %bitcast.1.len_ref, bf16[512,2304]{1,0:T(8,128)(2,1)} %fusion.40.q_ref.k_ref.v_ref, bf16[512,2304]{1,0:T(8,128)(2,1)} %fusion.40.q_ref.k_ref.v_ref, bf16[512,2304]{1,0:T(8,128)(2,1)} %fusion.40.q_ref.k_ref.v_ref), custom_call_target="tpu_custom_call" | custom-call | flops 3221225472 | bytes 3145728 | tf_op jit(solution)/shard_map/attn_fwd/pallas_call | solution.py:73
  391.5 12.2 %fusion.191 = (f32[768]{0:T(1024)S(1)}, f32[512]{0:T(512)S(1)}, f32[512]{0:T(512)S(1)}, f32[768]{0:T(1024)S(1)}, bf16[512,768]{1,0:T(8,128)(2,1)}) fusion(bf16[512,768]{1,0:T(8,128)(2,1)} %get-tuple-element.308, f32[512]{0:T(512)S(1)} %add_rsqrt_fusion.1, f32[512]{0:T(512)S(1)} %broadcast_multiply_fusion.17, f32[768]{0:T(1024)S(1)} %copy-done.46, ...), kind=kOutput, calls=%fused_computation.308 | convolution fusion | flops 4857000960 | bytes 18117640 | tf_op jit(solution)/shard_map/dot_general | solution.py:21
  407.9 18.6 %attn_bwd.4 = bf16[512,2304]{1,0:T(8,128)(2,1)} custom-call(s32[1]{0:T(128)} %bitcast.1.len_ref, bf16[512,2304]{1,0:T(8,128)(2,1)} %fusion.40.q_ref.k_ref.v_ref, bf16[512,2304]{1,0:T(8,128)(2,1)} %fusion.40.q_ref.k_ref.v_ref, bf16[512,2304]{1,0:T(8,128)(2,1)} %fusion.40.q_ref.k_ref.v_ref, bf16[512,768]{1,0:T(8,128)(2,1)} %convolution_convert_fusion.8.dctx_ref), custom_call_target="tpu_custom_call" | custom-call | flops 8053063680 | bytes 5505024 | tf_op jit(solution)/shard_map/attn_bwd/pallas_call | solution.py:87
  436.2 12.3 %fusion.193 = (f32[768]{0:T(1024)S(1)}, f32[512]{0:T(512)S(1)}, f32[512]{0:T(512)S(1)}, f32[768]{0:T(1024)S(1)}, bf16[512,768]{1,0:T(8,128)(2,1)}) fusion(bf16[512,768]{1,0:T(8,128)(2,1)} %get-tuple-element.304, f32[512]{0:T(512)S(1)} %add_rsqrt_fusion.3, f32[512]{0:T(512)S(1)} %broadcast_multiply_fusion.19, f32[768]{0:T(1024)S(1)} %get-tuple-element.322, ...), kind=kOutput, calls=%fused_computation.310 | convolution fusion | flops 4857000960 | bytes 18117632 | tf_op jit(solution)/shard_map/dot_general | solution.py:21
  453.9 18.8 %attn_bwd.5 = bf16[512,2304]{1,0:T(8,128)(2,1)} custom-call(s32[1]{0:T(128)} %bitcast.1.len_ref, bf16[512,2304]{1,0:T(8,128)(2,1)} %fusion.39.q_ref.k_ref.v_ref, bf16[512,2304]{1,0:T(8,128)(2,1)} %fusion.39.q_ref.k_ref.v_ref, bf16[512,2304]{1,0:T(8,128)(2,1)} %fusion.39.q_ref.k_ref.v_ref, bf16[512,768]{1,0:T(8,128)(2,1)} %convolution_convert_fusion.7.dctx_ref), custom_call_target="tpu_custom_call" | custom-call | flops 8053063680 | bytes 5505024 | tf_op jit(solution)/shard_map/attn_bwd/pallas_call | solution.py:87
  491.3 11.7 %collective-permute-done.28 = bf16[512,768]{1,0:T(8,128)(2,1)} collective-permute-done((bf16[512,768]{1,0:T(8,128)(2,1)}, bf16[512,768]{1,0:T(8,128)(2,1)}, u32[]{:S(2)}, u32[]{:S(2)}) %collective-permute-start.28) | collective-permute-done | bytes 786464 | tf_op jit(solution)/shard_map/ppermute | solution.py:240
  503.0 12.4 %fusion.195 = (f32[768]{0:T(1024)S(1)}, f32[512]{0:T(512)S(1)}, f32[512]{0:T(512)S(1)}, f32[768]{0:T(1024)S(1)}, bf16[512,768]{1,0:T(8,128)(2,1)}) fusion(bf16[512,768]{1,0:T(8,128)(2,1)} %copy-done.25, f32[512]{0:T(512)S(1)} %add_rsqrt_fusion.5, f32[512]{0:T(512)S(1)} %broadcast_multiply_fusion.21, f32[768]{0:T(1024)S(1)} %copy-done.46, ...), kind=kOutput, calls=%fused_computation.312 | convolution fusion | flops 4857000960 | bytes 18117632 | tf_op jit(solution)/shard_map/dot_general | solution.py:21
  522.6 18.5 %attn_bwd.6 = bf16[512,2304]{1,0:T(8,128)(2,1)} custom-call(s32[1]{0:T(128)} %bitcast.1.len_ref, bf16[512,2304]{1,0:T(8,128)(2,1)} %fusion.38.q_ref.k_ref.v_ref, bf16[512,2304]{1,0:T(8,128)(2,1)} %fusion.38.q_ref.k_ref.v_ref, bf16[512,2304]{1,0:T(8,128)(2,1)} %fusion.38.q_ref.k_ref.v_ref, bf16[512,768]{1,0:T(8,128)(2,1)} %convolution_convert_fusion.6.dctx_ref), custom_call_target="tpu_custom_call" | custom-call | flops 8053063680 | bytes 5505024 | tf_op jit(solution)/shard_map/attn_bwd/pallas_call | solution.py:87
  561.8 12.0 %fusion.197 = (f32[768]{0:T(1024)S(1)}, f32[512]{0:T(512)S(1)}, f32[512]{0:T(512)S(1)}, f32[768]{0:T(1024)S(1)}, bf16[512,768]{1,0:T(8,128)(2,1)}) fusion(bf16[512,768]{1,0:T(8,128)(2,1)} %get-tuple-element.298, f32[512]{0:T(512)S(1)} %copy-done.73, f32[512]{0:T(512)S(1)} %copy-done.53, f32[768]{0:T(1024)S(1)} %get-tuple-element.322, ...), kind=kOutput, calls=%fused_computation.314 | convolution fusion | flops 4857000960 | bytes 18117632 | tf_op jit(solution)/shard_map/dot_general | solution.py:21
  578.4 18.4 %attn_bwd.7 = bf16[512,2304]{1,0:T(8,128)(2,1)} custom-call(s32[1]{0:T(128)} %bitcast.1.len_ref, bf16[512,2304]{1,0:T(8,128)(2,1)} %fusion.37.q_ref.k_ref.v_ref, bf16[512,2304]{1,0:T(8,128)(2,1)} %fusion.37.q_ref.k_ref.v_ref, bf16[512,2304]{1,0:T(8,128)(2,1)} %fusion.37.q_ref.k_ref.v_ref, bf16[512,768]{1,0:T(8,128)(2,1)} %convolution_convert_fusion.5.dctx_ref), custom_call_target="tpu_custom_call" | custom-call | flops 8053063680 | bytes 5505024 | tf_op jit(solution)/shard_map/attn_bwd/pallas_call | solution.py:87
  655.2 25.0 %concatenate.48 = f32[4,784,768]{2,1,0:T(8,128)} concatenate(f32[4,192,768]{2,1,0:T(8,128)} %bitcast.412, f32[4,192,768]{2,1,0:T(8,128)S(1)} %bitcast.368, f32[4,5,768]{2,1,0:T(8,128)S(1)} %broadcast_in_dim.177, f32[4,3,768]{2,1,0:T(4,128)S(1)} %pad.13.clone, f32[4,392,768]{2,1,0:T(8,128)} %select_maximum_fusion), dimensions={1} | concatenate | bytes 19267584 | tf_op jit(solution)/shard_map/concatenate | solution.py:284
  707.6 58.0 %collective-permute-done.36 = bf16[4,512,768]{2,1,0:T(8,128)(2,1)} collective-permute-done((bf16[4,512,768]{2,1,0:T(8,128)(2,1)}, bf16[4,512,768]{2,1,0:T(8,128)(2,1)}, u32[]{:S(2)}, u32[]{:S(2)}) %collective-permute-start.36) | collective-permute-done | bytes 3145760 | tf_op jit(solution)/shard_map/ppermute | solution.py:240
  858.7 17.9 %collective-permute-done.39 = bf16[4,2,512,768]{3,2,0,1:T(8,128)(2,1)} collective-permute-done((bf16[4,2,512,768]{3,2,0,1:T(8,128)(2,1)}, bf16[4,2,512,768]{3,2,0,1:T(8,128)(2,1)}, u32[]{:S(2)}, u32[]{:S(2)}) %collective-permute-start.39) | collective-permute-done | bytes 6291488 | tf_op jit(solution)/shard_map/ppermute | solution.py:289
  883.4 13.0 %fusion.312 = (f32[768]{0:T(1024)S(1)}, bf16[4096,768]{1,0:T(8,128)(2,1)}) fusion(f32[4096,768]{1,0:T(8,128)} %fusion.207, f32[768]{0:T(1024)S(1)} %reduce.20, bf16[4096,768]{1,0:T(8,128)(2,1)S(1)} %bitcast.374, bf16[1,768,768]{2,1,0:T(8,128)(2,1)S(1)} %copy-done.45), kind=kOutput, calls=%fused_computation.546 | convolution fusion | flops 4875877376 | bytes 26351616 | tf_op jit(solution)/shard_map/dot_general | solution.py:21
  907.5 27.9 %reduce-scatter.2.cloned.1.call-done = f32[1,784,768]{2,1,0:T(8,128)} async-done(((f32[4,784,768]{2,1,0:T(8,128)}), f32[1,784,768]{2,1,0:T(8,128)}) %reduce-scatter.2.cloned.1.call-update) | async-done | bytes 2408464 | tf_op jit(solution)/shard_map/reduce_scatter | solution.py:285
  (541 shorter events, 512.3 us)
Async XLA Ops:
  12.1 84.1 %all-gather.22.cloned.1.call-start = ((), (), s32[]{:S(2)}) async-start(), calls=%async_computation.3 | async-start | bytes 2949120 | tf_op jit(solution)/shard_map/all_gather | solution.py:178
  17.8 149.6 %all-gather.26.cloned.1.call-start = ((), (), s32[]{:S(2)}) async-start(), calls=%async_computation.5 | async-start | bytes 4423680 | tf_op jit(solution)/shard_map/all_gather | solution.py:178
  64.6 562.3 %all-gather.24.cloned.1.call-start = ((), (), s32[]{:S(2)}) async-start(), calls=%async_computation.4 | async-start | bytes 3932160 | tf_op jit(solution)/shard_map/all_gather | solution.py:178
  173.0 51.6 %collective-permute-start.18 = (bf16[4,192,768]{2,1,0:T(8,128)(2,1)S(1)}, bf16[4,192,768]{2,1,0:T(8,128)(2,1)}, u32[]{:S(2)}, u32[]{:S(2)}) collective-permute-start(bf16[4,192,768]{2,1,0:T(8,128)(2,1)S(1)} %get-tuple-element.120), channel_id=1, source_target_pairs={{0,16},{16,0},{1,17},{17,1},{2,18},{18,2},{3,19},{19,3},{4,20},{20... | collective-permute-start | bytes 3538952 | tf_op jit(solution)/shard_map/ppermute | solution.py:207
  173.2 79.9 %collective-permute-start.20 = (bf16[4,192,768]{2,1,0:T(8,128)(2,1)S(1)}, bf16[4,192,768]{2,1,0:T(8,128)(2,1)}, u32[]{:S(2)}, u32[]{:S(2)}) collective-permute-start(bf16[4,192,768]{2,1,0:T(8,128)(2,1)S(1)} %get-tuple-element.128), channel_id=1, source_target_pairs={{0,1},{1,0},{2,3},{3,2},{4,5},{5,4},{6,7},{7,6},{8,9},{9,8},{10,11... | collective-permute-start | bytes 3538952 | tf_op jit(solution)/shard_map/ppermute | solution.py:181
  193.2 56.7 %collective-permute-start.21 = (bf16[4,192,768]{2,1,0:T(8,128)(2,1)S(1)}, bf16[4,192,768]{2,1,0:T(8,128)(2,1)}, u32[]{:S(2)}, u32[]{:S(2)}) collective-permute-start(bf16[4,192,768]{2,1,0:T(8,128)(2,1)S(1)} %get-tuple-element.128), channel_id=1, source_target_pairs={{0,16},{16,0},{1,17},{17,1},{2,18},{18,2},{3,19},{19,3},{4,20},{20... | collective-permute-start | bytes 3538952 | tf_op jit(solution)/shard_map/ppermute | solution.py:207
  201.8 107.8 %collective-permute-start.5 = (bf16[512,768]{1,0:T(8,128)(2,1)}, bf16[512,768]{1,0:T(8,128)(2,1)}, u32[]{:S(2)}, u32[]{:S(2)}) collective-permute-start(bf16[512,768]{1,0:T(8,128)(2,1)} %get-tuple-element.298), channel_id=1, source_target_pairs={{0,2},{1,3},{4,6},{5,7},{8,10},{9,11},{12,14},{13,15},{16,18},{17,... | collective-permute-start | bytes 2359304 | tf_op jit(solution)/shard_map/ppermute | solution.py:240
  206.0 55.7 %collective-permute-start.16 = (bf16[4,192,768]{2,1,0:T(8,128)(2,1)}, bf16[4,192,768]{2,1,0:T(8,128)(2,1)}, u32[]{:S(2)}, u32[]{:S(2)}) collective-permute-start(bf16[4,192,768]{2,1,0:T(8,128)(2,1)} %collective-permute-done.15), channel_id=1, source_target_pairs={{0,1},{1,0},{2,3},{3,2},{4,5},{5,4},{6,7},{7,6},{8,9},{9,8},{10,11... | collective-permute-start | bytes 3538952 | tf_op jit(solution)/shard_map/ppermute | solution.py:181
  310.6 321.4 %all-gather.30.cloned.1.call-start = ((), (), s32[]{:S(2)}) async-start(), calls=%async_computation.7 | async-start | bytes 3932160 | tf_op jit(solution)/shard_map/all_gather | solution.py:178
  310.7 93.1 %collective-permute-start.25 = (bf16[512,768]{1,0:T(8,128)(2,1)S(1)}, bf16[512,768]{1,0:T(8,128)(2,1)}, u32[]{:S(2)}, u32[]{:S(2)}) collective-permute-start(bf16[512,768]{1,0:T(8,128)(2,1)S(1)} %get-tuple-element.302), channel_id=1, source_target_pairs={{0,2},{1,3},{4,6},{5,7},{8,10},{9,11},{12,14},{13,15},{16,18},{17,... | collective-permute-start | bytes 2359304 | tf_op jit(solution)/shard_map/ppermute | solution.py:240
  346.7 142.3 %collective-permute-start.24 = (bf16[512,768]{1,0:T(8,128)(2,1)}, bf16[512,768]{1,0:T(8,128)(2,1)}, u32[]{:S(2)}, u32[]{:S(2)}) collective-permute-start(bf16[512,768]{1,0:T(8,128)(2,1)} %get-tuple-element.304), channel_id=1, source_target_pairs={{2,0},{3,1},{6,4},{7,5},{10,8},{11,9},{14,12},{15,13},{18,16},{19,... | collective-permute-start | bytes 2359304 | tf_op jit(solution)/shard_map/ppermute | solution.py:240
  380.5 108.4 %collective-permute-start.26 = (bf16[512,768]{1,0:T(8,128)(2,1)}, bf16[512,768]{1,0:T(8,128)(2,1)}, u32[]{:S(2)}, u32[]{:S(2)}) collective-permute-start(bf16[512,768]{1,0:T(8,128)(2,1)} %get-tuple-element.308), channel_id=1, source_target_pairs={{2,0},{3,1},{6,4},{7,5},{10,8},{11,9},{14,12},{15,13},{18,16},{19,... | collective-permute-start | bytes 2359304 | tf_op jit(solution)/shard_map/ppermute | solution.py:240
  448.5 184.8 %all-gather.32.cloned.1.call-start = ((), (), s32[]{:S(2)}) async-start(), calls=%async_computation.8 | async-start | bytes 3932160 | tf_op jit(solution)/shard_map/all_gather | solution.py:178
  491.1 151.4 %all-gather.28.cloned.1.call-start = ((), (), s32[]{:S(2)}) async-start(), calls=%async_computation.6 | async-start | bytes 3932160 | tf_op jit(solution)/shard_map/all_gather | solution.py:178
  547.0 159.7 %all-gather.36.cloned.1.call-start = ((), (), s32[]{:S(2)}) async-start(), calls=%async_computation.10 | async-start | bytes 3932160 | tf_op jit(solution)/shard_map/all_gather | solution.py:178
  573.8 196.6 %all-gather.34.cloned.1.call-start = ((), (), s32[]{:S(2)}) async-start(), calls=%async_computation.9 | async-start | bytes 3932160 | tf_op jit(solution)/shard_map/all_gather | solution.py:178
  615.5 319.8 %reduce-scatter.2.cloned.1.call-start = ((), (), s32[]{:S(2)}) async-start(), calls=%async_computation.1 | async-start | bytes 12042240 | tf_op jit(solution)/shard_map/reduce_scatter | solution.py:285
  626.9 71.2 %collective-permute-start.34 = (bf16[4,512,768]{2,1,0:T(8,128)(2,1)}, bf16[4,512,768]{2,1,0:T(8,128)(2,1)}, u32[]{:S(2)}, u32[]{:S(2)}) collective-permute-start(bf16[4,512,768]{2,1,0:T(8,128)(2,1)} %bitcast.397), channel_id=1, source_target_pairs={{2,0},{3,1},{6,4},{7,5},{10,8},{11,9},{14,12},{15,13},{18,16},{19,... | collective-permute-start | bytes 9437192 | tf_op jit(solution)/shard_map/ppermute | solution.py:240
  632.0 133.5 %collective-permute-start.36 = (bf16[4,512,768]{2,1,0:T(8,128)(2,1)}, bf16[4,512,768]{2,1,0:T(8,128)(2,1)}, u32[]{:S(2)}, u32[]{:S(2)}) collective-permute-start(bf16[4,512,768]{2,1,0:T(8,128)(2,1)} %bitcast.399), channel_id=1, source_target_pairs={{2,0},{3,1},{6,4},{7,5},{10,8},{11,9},{14,12},{15,13},{18,16},{19,... | collective-permute-start | bytes 9437192 | tf_op jit(solution)/shard_map/ppermute | solution.py:240
  633.3 137.9 %collective-permute-start.37 = (bf16[4,512,768]{2,1,0:T(8,128)(2,1)}, bf16[4,512,768]{2,1,0:T(8,128)(2,1)}, u32[]{:S(2)}, u32[]{:S(2)}) collective-permute-start(bf16[4,512,768]{2,1,0:T(8,128)(2,1)} %bitcast.401), channel_id=1, source_target_pairs={{0,2},{1,3},{4,6},{5,7},{8,10},{9,11},{12,14},{13,15},{16,18},{17,... | collective-permute-start | bytes 9437192 | tf_op jit(solution)/shard_map/ppermute | solution.py:240
  642.5 132.4 %collective-permute-start.35 = (bf16[4,512,768]{2,1,0:T(8,128)(2,1)}, bf16[4,512,768]{2,1,0:T(8,128)(2,1)}, u32[]{:S(2)}, u32[]{:S(2)}) collective-permute-start(bf16[4,512,768]{2,1,0:T(8,128)(2,1)} %bitcast.403), channel_id=1, source_target_pairs={{0,2},{1,3},{4,6},{5,7},{8,10},{9,11},{12,14},{13,15},{16,18},{17,... | collective-permute-start | bytes 9437192 | tf_op jit(solution)/shard_map/ppermute | solution.py:240
  687.5 95.0 %collective-permute-start.27 = (bf16[4,512,768]{2,1,0:T(8,128)(2,1)}, bf16[4,512,768]{2,1,0:T(8,128)(2,1)}, u32[]{:S(2)}, u32[]{:S(2)}) collective-permute-start(bf16[4,512,768]{2,1,0:T(8,128)(2,1)} %get-tuple-element.253), channel_id=1, source_target_pairs={{0,1},{1,0},{2,3},{3,2},{4,5},{5,4},{6,7},{7,6},{8,9},{9,8},{10,11... | collective-permute-start | bytes 9437192 | tf_op jit(solution)/shard_map/ppermute | solution.py:181
  706.7 82.5 %collective-permute-start.31 = (bf16[4,512,768]{2,1,0:T(8,128)(2,1)}, bf16[4,512,768]{2,1,0:T(8,128)(2,1)}, u32[]{:S(2)}, u32[]{:S(2)}) collective-permute-start(bf16[4,512,768]{2,1,0:T(8,128)(2,1)} %bitcast.405), channel_id=1, source_target_pairs={{0,1},{1,0},{2,3},{3,2},{4,5},{5,4},{6,7},{7,6},{8,9},{9,8},{10,11... | collective-permute-start | bytes 9437192 | tf_op jit(solution)/shard_map/ppermute | solution.py:181
  803.7 72.9 %collective-permute-start.39 = (bf16[4,2,512,768]{3,2,0,1:T(8,128)(2,1)}, bf16[4,2,512,768]{3,2,0,1:T(8,128)(2,1)}, u32[]{:S(2)}, u32[]{:S(2)}) collective-permute-start(bf16[4,2,512,768]{3,2,0,1:T(8,128)(2,1)} %pad_maximum_fusion.1), channel_id=1, source_target_pairs={{2,1},{6,5},{10,9},{14,13},{18,17},{22,21},{26,25},{30,29}} | collective-permute-start | bytes 18874376 | tf_op jit(solution)/shard_map/ppermute | solution.py:289
  (120 other events, 1780.3 us)
Sparse Core Ops, SparseCore 0:
  12.2 31.7 all-gather.19
  46.1 50.0 all-gather.21
  98.4 68.9 all-gather.25
  310.8 60.5 all-gather.23
  448.7 66.5 all-gather.29
  516.7 62.0 all-gather.31
  580.3 62.0 all-gather.27
  644.6 62.0 all-gather.35
  708.3 62.0 all-gather.33
  772.6 162.6 reduce-scatter.1
